TPU v7x, 32 devices: a whole 2x2x4 slice. The times are simulated.
32 devices in a mesh: dp: 8 (over z, y), mp: 4 (over x, core).
Axes of the slice: x: 2, y: 2, z: 4, core: 2. Of those that a mesh axis runs over, the one named last changes fastest.
Arguments:
- gradient: bfloat16 [1, 4096, 4096], P(None, 'mp', 'dp'), may hold values from -6 to 6
- first_moment: float32 [1, 4096, 4096], P(None, 'mp', 'dp'), may hold values from -3 to 3
- second_moment: float32 [1, 4096, 4096], P(None, 'mp', 'dp'), may hold values from 0.0625 to 1
- left_factor: float32 [1, 4096, 4096], P(None, 'mp', 'dp'), may hold values from -18 to 18
- right_factor: float32 [1, 4096, 4096], P(None, 'mp', 'dp'), may hold values from -18 to 18
- left_basis: bfloat16 [1, 4096, 4096], P(None, 'dp', 'mp'), may hold values from -0.09375 to 0.09375
- right_basis: bfloat16 [1, 4096, 4096], P(None, 'mp', 'dp'), may hold values from -0.09375 to 0.09375
Outputs:
- new_first_moment: float32 [1, 4096, 4096], P(None, 'mp', 'dp')
- new_second_moment: float32 [1, 4096, 4096], P(None, 'mp', 'dp')
- new_left_factor: float32 [1, 4096, 4096], P(None, 'mp', 'dp')
- new_right_factor: float32 [1, 4096, 4096], P(None, 'mp', 'dp')
- update: bfloat16 [1, 4096, 4096], P(None, 'mp', 'dp')
All inputs are finite; a program needn't handle non-finite values.
Results may differ from a plain program's by a relative error of at most 0.014.
Values may be sent and summed in bfloat16 or wider, within the bound.
A program may use at most 128 MiB of HBM per device.

v0:
```python
import functools

import jax
import jax.numpy as jnp
from jax import lax
from jax.experimental import pallas as pl
from jax.experimental.pallas import tpu as pltpu
from jax.sharding import PartitionSpec as P

decay_moment = 0.95
decay_factor = 0.95
epsilon = 1e-08
bf16, f32 = jnp.bfloat16, jnp.float32
MESH = pl.DeviceIdType.MESH


def kernel(dp, mp, rows, cols, chunks, *refs):
    (grad, first, second, left_f, right_f, left_b, right_b,
     out_first, out_second, out_left, out_right, out_update,
     gbuf, lbuf, rbuf, rrbuf, pbuf, ssend, rrecv, urecv, yrecv, zrecv,
     fac_l, fac_r, mom1, mom2, acc, dbuf, bbuf,
     load_sem, store_sem, zs_up, zs_dn, zr, ys, yr, es, er, as_, ar,
     rs, rr, us, ur, ps, pr, bys, byr, bzs, bzr) = refs
    Z, q = dp // 2, rows // cols
    cw = cols // chunks
    d, m = lax.axis_index("dp"), lax.axis_index("mp")
    z, y = lax.div(d, 2), lax.rem(d, 2)
    last = Z - 1
    ynbr = z * 2 + (1 - y)
    tile = min(256, rows)

    def send(src, dst, s, r, dev):
        return pltpu.make_async_remote_copy(
            src_ref=src, dst_ref=dst, send_sem=s, recv_sem=r, device_id=dev, device_id_type=MESH
        )

    def when(cond, fn):
        pl.when(cond)(fn)

    def loop(n, fn):
        def body(i, c):
            fn(i)
            return c
        lax.fori_loop(0, n, body, 0)

    def tiles(n, size, fn):
        loop(n // size, lambda i: fn(pl.ds(pl.multiple_of(i * size, size), size)))

    loads = [
        (grad, gbuf.at[d]), (left_b, lbuf.at[d]), (right_b, rbuf.at[m]),
        (first, mom1), (second, mom2), (left_f, fac_l), (right_f, fac_r),
    ]
    load = [pltpu.make_async_copy(a, b, load_sem.at[i]) for i, (a, b) in enumerate(loads)]
    for c in load:
        c.start()

    barrier = pltpu.get_barrier_semaphore()
    pl.semaphore_signal(barrier, inc=1, device_id=(ynbr, m), device_id_type=MESH)
    when(z > 0, lambda: pl.semaphore_signal(barrier, inc=1, device_id=(d - 2, m), device_id_type=MESH))
    when(z < last, lambda: pl.semaphore_signal(barrier, inc=1, device_id=(d + 2, m), device_id_type=MESH))
    for k in range(1, mp):
        pl.semaphore_signal(barrier, inc=1, device_id=(d, lax.rem(m + k, mp)), device_id_type=MESH)
    along = (z > 0).astype(jnp.int32) + (z < last).astype(jnp.int32)
    pl.semaphore_wait(barrier, mp + along)

    bufs = [gbuf, lbuf]

    def half(a, b, hb):
        n = bufs[a].shape[1] // 2
        return bufs[a].at[b, pl.ds(hb * n, n), :]

    def up(a, zb):
        blk = bufs[a].at[zb * 2 + y]
        return send(blk, blk, zs_up.at[a, zb], zr.at[a, zb], (d + 2, m))

    def dn(a, zb):
        blk = bufs[a].at[zb * 2 + y]
        return send(blk, blk, zs_dn.at[a, zb], zr.at[a, zb], (d - 2, m))

    def ysend(a, zb, hb):
        blk = half(a, zb * 2 + y, hb)
        return send(blk, blk, ys.at[a, zb, hb], yr.at[a, zb, hb], (ynbr, m))

    def yrecv_desc(a, zb, hb):
        blk = half(a, zb * 2 + (1 - y), hb)
        return send(blk, blk, ys.at[a, zb, hb], yr.at[a, zb, hb], (ynbr, m))

    def extra(a, k):
        zb = 0 if k == 0 else last
        blk = half(a, zb * 2 + (1 - y), 1)
        return send(blk, blk, es.at[a, k], er.at[a, k], (d + 2, m) if k == 0 else (d - 2, m))

    def in_line(zb):
        return jnp.logical_and(zb >= 0, zb <= last)

    def y_second(zb):
        inner = jnp.logical_and(zb > 0, zb < last)
        return jnp.logical_or(zb == z, inner)

    def y_sends(a, zb, op):
        op(ysend(a, zb, 0))
        when(y_second(zb), lambda: op(ysend(a, zb, 1)))

    def start(c):
        c.start()

    def ag_up_own(a):
        when(z < last, lambda: up(a, z).start())

    def ag_dn_own(a):
        when(z > 0, lambda: dn(a, z).start())

    def ag_step(a, s, then, on_block):
        below, above = z - s, z + s

        def from_below():
            up(a, below).wait_recv()
            when(z < last, lambda: up(a, below).start())

        def from_above():
            dn(a, above).wait_recv()
            when(z > 0, lambda: dn(a, above).start())

        when(below >= 0, from_below)
        if then:
            when(z == s, lambda: ag_up_own(1))
        when(above <= last, from_above)
        if then:
            when(last - z == s, lambda: ag_dn_own(1))
        when(below >= 0, lambda: y_sends(a, below, start))
        when(above <= last, lambda: y_sends(a, above, start))

        def extra_dn():
            when(z == last, lambda: yrecv_desc(a, z, 1).wait_recv())
            when(z < last, lambda: extra(a, 1).wait_recv())
            extra(a, 1).start()

        def extra_up():
            when(z == 0, lambda: yrecv_desc(a, z, 1).wait_recv())
            when(z > 0, lambda: extra(a, 0).wait_recv())
            extra(a, 0).start()

        when(jnp.logical_and(z == Z - s, z > 0), extra_dn)
        when(jnp.logical_and(z == s - 1, z < last), extra_up)
        if on_block is not None:
            when(below >= 0, lambda: on_block(below * 2 + y))
            when(above <= last, lambda: on_block(above * 2 + y))

    def wait_y(a, zb):
        yrecv_desc(a, zb, 0).wait_recv()
        inner = jnp.logical_and(zb > 0, zb < last)
        when(inner, lambda: yrecv_desc(a, zb, 1).wait_recv())
        when(jnp.logical_and(zb == last, z == 0), lambda: extra(a, 1).wait_recv())
        when(jnp.logical_and(zb == 0, z == last), lambda: extra(a, 0).wait_recv())

    def by_distance(fn, far_first=False):
        def step(i):
            s = last - i if far_first else i
            when(z - s >= 0, lambda: fn(z - s))
            when(jnp.logical_and(s > 0, z + s <= last), lambda: fn(z + s))
        loop(Z, step)

    def sub_rows(ref, db):
        off = pl.multiple_of(lax.rem(db, q) * cols, cols)
        return ref.at[lax.div(db, q), pl.ds(off, cols), :]

    def mp_send(a, buf, k):
        to = lax.rem(m + k, mp)
        return send(buf.at[m], buf.at[m], as_.at[a, k], ar.at[a, m], (d, to))

    def mp_wait(a, buf):
        for k in range(1, mp):
            src = lax.rem(m + k, mp)
            send(buf.at[src], buf.at[src], as_.at[a, k], ar.at[a, src], (d, src)).wait_recv()

    load[0].wait()
    when(z < last, lambda: up(0, z).start())
    when(z > 0, lambda: dn(0, z).start())
    y_sends(0, z, start)
    load[2].wait()
    for k in range(1, mp):
        mp_send(0, rbuf, k).start()
    load[1].wait()
    when(z == 0, lambda: ag_up_own(1))
    when(z == last, lambda: ag_dn_own(1))

    def r_send(db):
        to, sub = lax.div(db, q), lax.rem(db, q)
        return send(ssend.at[db], rrecv.at[m, sub], rs.at[db], rr.at[m, sub], (d, to))

    def r_term(db):
        def one(t):
            term = lax.dot_general(
                gbuf[db, :, t], gbuf[d], (((0,), (0,)), ((), ())), preferred_element_type=f32
            )
            ssend[db, t, :] = term.astype(bf16)
        tiles(cols, min(256, cols), one)
        when(lax.div(db, q) != m, lambda: r_send(db).start())

    def rr_term(db):
        rhs = sub_rows(rbuf, db)
        def one(t):
            acc[t, :] += jnp.dot(gbuf[db, t, :], rhs[...], preferred_element_type=f32)
        tiles(rows, tile, one)

    def zero_acc():
        def one(t):
            acc[t, :] = jnp.zeros((tile, cols), f32)
        tiles(rows, tile, one)

    r_term(d)
    loop(Z - 1, lambda i: ag_step(0, i + 1, True, r_term))
    y_sends(1, z, start)
    zero_acc()
    mp_wait(0, rbuf)
    by_distance(lambda zb: rr_term(zb * 2 + y))

    def y_block(zb):
        wait_y(0, zb)
        rr_term(zb * 2 + 1 - y)
        r_term(zb * 2 + 1 - y)
    by_distance(y_block)

    def rr_out(t):
        rrbuf[m, t, :] = acc[t, :].astype(bf16)
    tiles(rows, tile, rr_out)
    for k in range(1, mp):
        mp_send(1, rrbuf, k).start()

    owner = lax.div(d, q)
    core, chip = lax.rem(m, 2), lax.div(m, 2)
    own_chip, own_core = lax.div(owner, 2), lax.rem(owner, 2)
    partner = chip * 2 + (1 - core)
    hd = dp // 2
    pair_off = pl.multiple_of(lax.rem(d, q) * cols, cols)

    def p_send(hb, i, to):
        part = pbuf.at[pl.ds(hb * hd, hd)]
        return send(part, part, ps.at[i], pr.at[hb], (d, to))

    def to_chips(op):
        for k in range(1, mp // 2):
            other = lax.rem(chip + k, mp // 2)
            op(p_send(core, 2 + k, other * 2 + core))

    def own_pair():
        def copy(i):
            pbuf[i] = gbuf[i, pl.ds(pair_off, cols), :]
        loop(dp, copy)
        for hb in range(2):
            p_send(hb, hb, partner).start()
        to_chips(start)
    when(m == owner, own_pair)

    loop(Z - 1, lambda i: ag_step(1, i + 1, False, None))

    def near_pair():
        for hb in range(2):
            p_send(hb, hb, partner).wait_recv()
        to_chips(start)
    when(jnp.logical_and(chip == own_chip, m != owner), near_pair)

    mp_wait(1, rrbuf)
    zero_acc()

    def m_term(db):
        rhs = sub_rows(rrbuf, db)
        def one(t):
            acc[t, :] += lax.dot_general(
                lbuf[db, :, t], rhs[...], (((0,), (0,)), ((), ())), preferred_element_type=f32
            )
        tiles(rows, tile, one)
    by_distance(lambda zb: m_term(zb * 2 + y))

    def y_block2(zb):
        wait_y(1, zb)
        m_term(zb * 2 + 1 - y)
    by_distance(y_block2)
    load[3].wait()
    load[4].wait()

    def moments(t):
        rot = acc[t, :]
        new1 = decay_moment * mom1[t, :] + (1.0 - decay_moment) * rot
        new2 = decay_moment * mom2[t, :] + (1.0 - decay_moment) * rot * rot
        mom1[t, :] = new1
        mom2[t, :] = new2
        dbuf[t, :] = (new1 / (jnp.sqrt(new2) + epsilon)).astype(bf16)
    tiles(rows, min(128, rows), moments)

    def lanes(h):
        return pl.ds(h * cw, cw)

    def back_term(db, h, t):
        off = pl.multiple_of(lax.rem(db, q) * cols + h * cw, cw)
        rhs = rbuf[lax.div(db, q), pl.ds(off, cw), :]
        return lax.dot_general(
            dbuf[t, :], rhs, (((1,), (1,)), ((), ())), preferred_element_type=f32
        )

    def by_send(h, zb):
        return send(rrbuf.at[zb, :, lanes(h)], yrecv.at[h, zb], bys.at[h, zb], byr.at[h, zb], (ynbr, m))

    for k in range(1, mp):
        mp_send(1, rrbuf, k).wait_send()
    for h in range(chunks):
        def first_half(zb, h=h):
            def one(t):
                rrbuf[zb, t, lanes(h)] = back_term(zb * 2 + 1 - y, h, t).astype(bf16)
            tiles(rows, tile, one)
            by_send(h, zb).start()
        by_distance(first_half, far_first=True)

    stores = [
        pltpu.make_async_copy(a, b, store_sem.at[i])
        for i, (a, b) in enumerate([
            (mom1, out_first), (mom2, out_second), (fac_l, out_left), (fac_r, out_right), (dbuf, out_update)
        ])
    ]
    stores[0].start()
    stores[1].start()

    def far_pair():
        p_send(core, 0, partner).wait_recv()
        p_send(core, 0, partner).start()
        p_send(1 - core, 0, partner).wait_recv()
    when(chip != own_chip, far_pair)
    load[5].wait()
    load[6].wait()

    def r_final():
        for k in range(1, mp):
            src = lax.rem(m + k, mp)
            for sub in range(q):
                send(ssend.at[sub], rrecv.at[src, sub], rs.at[sub], rr.at[src, sub], (d, src)).wait_recv()
        for sub in range(q):
            def one(t, sub=sub):
                total = ssend[m * q + sub, t, :].astype(f32)
                for k in range(1, mp):
                    total += rrecv[lax.rem(m + k, mp), sub, t, :].astype(f32)
                where = pl.ds(pl.multiple_of(sub * cols + t.start, 128), 128)
                fac_r[where, :] = decay_factor * fac_r[where, :] + (1.0 - decay_factor) * total
            tiles(cols, 128, one)
    r_final()
    stores[3].start()

    def l_scale(t):
        fac_l[t, :] = decay_factor * fac_l[t, :]
    tiles(rows, tile, l_scale)

    def l_term(db):
        def one(t):
            fac_l[t, :] += (1.0 - decay_factor) * lax.dot_general(
                gbuf[db, t, :], pbuf[db], (((1,), (1,)), ((), ())), preferred_element_type=f32
            )
        tiles(rows, tile, one)
    loop(dp, l_term)
    stores[2].start()
    loop(dp, lambda db: when(lax.div(db, q) != m, lambda: r_send(db).wait_send()))

    def bz_up(h, zb):
        return send(yrecv.at[h, zb], zrecv.at[h, zb], bzs.at[h, zb], bzr.at[h, zb], (d + 2, m))

    def bz_dn(h, zb):
        slot = jnp.where(zb == z - 1, Z, zb)
        return send(yrecv.at[h, zb], zrecv.at[h, slot], bzs.at[h, zb], bzr.at[h, slot], (d - 2, m))

    def bz_wait(h, slot):
        send(zrecv.at[h, slot], zrecv.at[h, slot], bzs.at[h, 0], bzr.at[h, slot], (ynbr, m)).wait_recv()

    def u_send(h, db):
        to, sub = lax.div(db, q), lax.rem(db, q)
        return send(
            ssend.at[db, :, lanes(h)],
            urecv.at[m, sub, :, lanes(h)], us.at[h, db], ur.at[h, m, sub], (d, to),
        )

    for h in range(chunks):
        def line(zb, h=h):
            by_send(h, zb).wait_recv()

            def one(t):
                acc[t, lanes(0)] = back_term(zb * 2 + y, h, t) + yrecv[h, zb, t, :].astype(f32)
            tiles(rows, tile, one)

            def add(slot):
                bz_wait(h, slot)
                def more(t):
                    acc[t, lanes(0)] += zrecv[h, slot, t, :].astype(f32)
                tiles(rows, tile, more)
            when(jnp.logical_and(zb >= z, z > 0), lambda: add(zb))
            when(jnp.logical_and(zb < z, z < last), lambda: add(zb))
            when(jnp.logical_and(zb == z, z < last), lambda: add(Z))

            def pack(t):
                yrecv[h, zb, t, :] = acc[t, lanes(0)].astype(bf16)

            def keep(t):
                bbuf[t, lanes(h)] = acc[t, lanes(0)].astype(bf16)
            when(zb != z, lambda: tiles(rows, tile, pack))
            when(zb > z, lambda: bz_up(h, zb).start())
            when(zb < z, lambda: bz_dn(h, zb).start())
            when(zb == z, lambda: tiles(rows, tile, keep))
        by_distance(line, far_first=True)

        def u_term(i, h=h):
            db = lax.rem(m * q + dp // 2 + i, dp)
            ssend[db, :, lanes(h)] = jnp.dot(
                lbuf[db], bbuf[:, lanes(h)], preferred_element_type=f32
            ).astype(bf16)
            when(lax.div(db, q) != m, lambda: u_send(h, db).start())
        loop(dp, u_term)

    for h in range(chunks):
        for k in range(1, mp):
            src = lax.rem(m + k, mp)
            for sub in range(q):
                dst = urecv.at[src, sub, :, lanes(h)]
                send(dst, dst, us.at[h, 0], ur.at[h, src, sub], (d, src)).wait_recv()
        for sub in range(q):
            def one(t, sub=sub, h=h):
                total = ssend[m * q + sub, t, lanes(h)].astype(f32)
                for k in range(1, mp):
                    total += urecv[lax.rem(m + k, mp), sub, t, lanes(h)].astype(f32)
                where = pl.ds(pl.multiple_of(sub * cols + t.start, 128), 128)
                dbuf[where, lanes(h)] = total.astype(bf16)
            tiles(cols, 128, one)
    stores[4].start()

    for a in range(2):
        def sent(i, a=a):
            when(jnp.logical_and(z < last, i <= z), lambda: up(a, i).wait_send())
            when(jnp.logical_and(z > 0, i >= z), lambda: dn(a, i).wait_send())
            y_sends(a, i, lambda c: c.wait_send())
        loop(Z, sent)
        when(z > 0, lambda a=a: extra(a, 1).wait_send())
        when(z < last, lambda a=a: extra(a, 0).wait_send())
    for k in range(1, mp):
        mp_send(0, rbuf, k).wait_send()

    def near_sent():
        to_chips(lambda c: c.wait_send())
    when(chip == own_chip, near_sent)

    def own_sent():
        for hb in range(2):
            p_send(hb, hb, partner).wait_send()
    when(m == owner, own_sent)
    when(chip != own_chip, lambda: p_send(core, 0, partner).wait_send())
    for h in range(chunks):
        def b_sent(i, h=h):
            by_send(h, i).wait_send()
            when(i != z, lambda: bz_up(h, i).wait_send())
        loop(Z, b_sent)
        loop(dp, lambda db, h=h: when(lax.div(db, q) != m, lambda: u_send(h, db).wait_send()))
    for c in stores:
        c.wait()


def solution(mesh):
    dp, mp = mesh.shape["dp"], mesh.shape["mp"]
    Z = dp // 2

    def per_device(*args):
        _, rows, cols = args[0].shape
        q = rows // cols
        chunks = 2
        cw = cols // chunks
        flat = [a.reshape(a.shape[1:]) for a in args]
        dma = pltpu.SemaphoreType.DMA
        outs = pl.pallas_call(
            functools.partial(kernel, dp, mp, rows, cols, chunks),
            out_shape=[jax.ShapeDtypeStruct((rows, cols), t) for t in (f32, f32, f32, f32, bf16)],
            in_specs=[pl.BlockSpec(memory_space=pl.ANY)] * 7,
            out_specs=[pl.BlockSpec(memory_space=pl.ANY)] * 5,
            scratch_shapes=[
                pltpu.VMEM((dp, rows, cols), bf16),
                pltpu.VMEM((dp, cols, rows), bf16),
                pltpu.VMEM((mp, rows, cols), bf16),
                pltpu.VMEM((mp, rows, cols), bf16),
                pltpu.VMEM((dp, cols, cols), bf16),
                pltpu.VMEM((dp, cols, cols), bf16),
                pltpu.VMEM((mp, q, cols, cols), bf16),
                pltpu.VMEM((mp, q, cols, cols), bf16),
                pltpu.VMEM((chunks, Z, rows, cw), bf16),
                pltpu.VMEM((chunks, Z + 1, rows, cw), bf16),
                pltpu.VMEM((rows, cols), f32),
                pltpu.VMEM((rows, cols), f32),
                pltpu.VMEM((rows, cols), f32),
                pltpu.VMEM((rows, cols), f32),
                pltpu.VMEM((rows, cols), f32),
                pltpu.VMEM((rows, cols), bf16),
                pltpu.VMEM((rows, cols), bf16),
                dma((7,)),
                dma((5,)),
                dma((2, Z)),
                dma((2, Z)),
                dma((2, Z)),
                dma((2, Z, 2)),
                dma((2, Z, 2)),
                dma((2, 2)),
                dma((2, 2)),
                dma((2, mp)),
                dma((2, mp)),
                dma((dp,)),
                dma((mp, q)),
                dma((chunks, dp)),
                dma((chunks, mp, q)),
                dma((2 + mp // 2,)),
                dma((2,)),
                dma((chunks, Z)),
                dma((chunks, Z)),
                dma((chunks, Z)),
                dma((chunks, Z + 1)),
            ],
            compiler_params=pltpu.CompilerParams(
                collective_id=0, has_side_effects=True, vmem_limit_bytes=67043328
            ),
        )(*flat)
        return tuple(o.reshape((1,) + o.shape) for o in outs)

    return jax.shard_map(
        per_device,
        mesh=mesh,
        in_specs=(P(None, "mp", "dp"),) * 5 + (P(None, "dp", "mp"), P(None, "mp", "dp")),
        out_specs=(P(None, "mp", "dp"),) * 5,
        check_vma=False,
    )
```

profile of v0, /device:TPU:12, one launch (start us, length us, event | category | flops | bytes accessed | tf_op | source)
XLA Modules:
  0.0 328.4 jit_solution(13957799662956106879)
XLA Ops:
  0.6 316.9 %shard_map.110 = (f32[1024,512]{1,0:T(8,128)}, f32[1024,512]{1,0:T(8,128)}, f32[1024,512]{1,0:T(8,128)}, f32[1024,512]{1,0:T(8,128)}, bf16[1024,512]{1,0:T(8,128)(2,1)}) custom-call(bf16[1024,512]{1,0:T(8,128)(2,1)} %bitcast.21, f32[1024,512]{1,0:T(8,128)} %bitcast.16, f32[1024,512]{1,0:T(8,128)} %bitcast.17, f32[1024,512]{1,0:T(8,128)} %bitcast.18, ...), custom_call_target="tpu_custom_call" | custom-call | tf_op jit(solution)/shard_map/pallas_call | solution.py:471
  317.5 0.0 copy-start.2
  317.5 3.2 copy.17
  320.7 0.0 copy-done.2
  320.7 0.0 copy-start.1
  320.7 1.3 copy.18
  322.1 1.0 copy-done.1
  323.1 0.0 copy-start
  323.1 1.3 copy.19
  324.4 1.0 copy-done
  325.4 0.0 copy-start.3
  325.4 1.3 copy.20
  326.8 0.6 copy-done.3
  327.4 1.0 copy.21
Async XLA Ops:
  317.5 3.2 copy-start.2
  320.7 2.3 copy-start.1
  323.1 2.3 copy-start
  325.4 2.0 copy-start.3
where the time goes:
time: 329 us; the launch traced here: 328 us
  Pallas kernels  317 us (96%)
  local copies, waits for them, and re-layouts  10.9 us (3%)
    pallas_call x1, Pallas kernels, per_device(): pl.pallas_call(functools.partial(kernel, dp, mp, rows, cols, chunks), out...  317 us
    unnamed x13, local copies, waits for them, and re-layouts  10.9 us

commit v1 on v0

v1 whole, which is shorter than its diff:
```python
import functools

import jax
import jax.numpy as jnp
from jax import lax
from jax.experimental import pallas as pl
from jax.experimental.pallas import tpu as pltpu
from jax.sharding import PartitionSpec as P

decay_moment = 0.95
decay_factor = 0.95
epsilon = 1e-08
bf16, f32 = jnp.bfloat16, jnp.float32
MESH = pl.DeviceIdType.MESH
PARTS, LAST = 2, 4


def kernel(dp, mp, rows, cols, parts, last_chunks, *refs):
    (grad, first, second, left_f, right_f, left_b, right_b,
     out_first, out_second, out_left, out_right, out_update,
     gbuf, lbuf, rbuf, rrbuf, pbuf, ssend, rrecv, urecv, ysrc, yrecv, zrecv,
     fac_l, fac_r, mom1, mom2, acc, dbuf, bbuf,
     load_sem, store_sem, zs_up, zs_dn, zr, ys, yr, es, er, as_, ar,
     rs, rr, us1, ur1, us2, ur2, ps, pr, bys, byr, bzs, bzr) = refs
    Z, q, X = dp // 2, rows // cols, mp // 2
    part = rows // parts
    d, m = lax.axis_index("dp"), lax.axis_index("mp")
    z, y = lax.div(d, 2), lax.rem(d, 2)
    core, chip = lax.rem(m, 2), lax.div(m, 2)
    partner = chip * 2 + (1 - core)
    last = Z - 1
    ynbr = z * 2 + (1 - y)
    tile = min(256, part)
    pieces = []
    for p in range(parts):
        n = last_chunks if p == parts - 1 else 1
        pieces.append([(p, i * (cols // n), cols // n) for i in range(n)])
    first_piece = [sum(len(x) for x in pieces[:p]) for p in range(parts)]

    def send(src, dst, s, r, dev):
        return pltpu.make_async_remote_copy(
            src_ref=src, dst_ref=dst, send_sem=s, recv_sem=r, device_id=dev, device_id_type=MESH
        )

    def when(cond, fn):
        pl.when(cond)(fn)

    def loop(n, fn):
        def body(i, c):
            fn(i)
            return c
        lax.fori_loop(0, n, body, 0)

    def tiles(n, size, fn, base=0):
        loop(n // size, lambda i: fn(pl.ds(pl.multiple_of(base + i * size, size), size)))

    loads = [
        (grad, gbuf.at[d]), (right_b, rbuf.at[m]),
        (first, mom1), (second, mom2), (left_f, fac_l), (right_f, fac_r),
    ]
    loads += [(left_b.at[:, pl.ds(p * part, part)], lbuf.at[p, d]) for p in range(parts)]
    load = [pltpu.make_async_copy(a, b, load_sem.at[i]) for i, (a, b) in enumerate(loads)]
    for c in load:
        c.start()

    barrier = pltpu.get_barrier_semaphore()
    pl.semaphore_signal(barrier, inc=1, device_id=(ynbr, m), device_id_type=MESH)
    when(z > 0, lambda: pl.semaphore_signal(barrier, inc=1, device_id=(d - 2, m), device_id_type=MESH))
    when(z < last, lambda: pl.semaphore_signal(barrier, inc=1, device_id=(d + 2, m), device_id_type=MESH))
    for k in range(1, mp):
        pl.semaphore_signal(barrier, inc=1, device_id=(d, lax.rem(m + k, mp)), device_id_type=MESH)
    along = (z > 0).astype(jnp.int32) + (z < last).astype(jnp.int32)
    pl.semaphore_wait(barrier, mp + along)

    def view(a, b):
        if a < 2:
            return gbuf.at[b, pl.ds(a * (rows // 2), rows // 2), :]
        return lbuf.at[a - 2, b]

    def half(a, b, hb):
        if a < 2:
            return gbuf.at[b, pl.ds(a * (rows // 2) + hb * (rows // 4), rows // 4), :]
        return lbuf.at[a - 2, b, pl.ds(hb * (cols // 2), cols // 2), :]

    def up(a, zb):
        blk = view(a, zb * 2 + y)
        return send(blk, blk, zs_up.at[a, zb], zr.at[a, zb], (d + 2, m))

    def dn(a, zb):
        blk = view(a, zb * 2 + y)
        return send(blk, blk, zs_dn.at[a, zb], zr.at[a, zb], (d - 2, m))

    def ysend(a, zb, hb):
        blk = half(a, zb * 2 + y, hb)
        return send(blk, blk, ys.at[a, zb, hb], yr.at[a, zb, hb], (ynbr, m))

    def yrecv_desc(a, zb, hb):
        blk = half(a, zb * 2 + (1 - y), hb)
        return send(blk, blk, ys.at[a, zb, hb], yr.at[a, zb, hb], (ynbr, m))

    def extra(a, k):
        zb = 0 if k == 0 else last
        blk = half(a, zb * 2 + (1 - y), 1)
        return send(blk, blk, es.at[a, k], er.at[a, k], (d + 2, m) if k == 0 else (d - 2, m))

    def y_second(zb):
        inner = jnp.logical_and(zb > 0, zb < last)
        return jnp.logical_or(zb == z, inner)

    def y_sends(a, zb, op):
        when(y_second(zb), lambda: op(ysend(a, zb, 1)))
        op(ysend(a, zb, 0))

    def start(c):
        c.start()

    def ag_own(a):
        when(z < last, lambda: up(a, z).start())
        when(z > 0, lambda: dn(a, z).start())

    def ag_step(a, s, then=None):
        below, above = z - s, z + s

        def from_below():
            up(a, below).wait_recv()
            when(z < last, lambda: up(a, below).start())

        def from_above():
            dn(a, above).wait_recv()
            when(z > 0, lambda: dn(a, above).start())

        when(below >= 0, from_below)
        when(above <= last, from_above)
        when(below >= 0, lambda: y_sends(a, below, start))
        when(above <= last, lambda: y_sends(a, above, start))

        def extra_dn():
            when(z == last, lambda: yrecv_desc(a, z, 1).wait_recv())
            when(z < last, lambda: extra(a, 1).wait_recv())
            extra(a, 1).start()
            if then is not None:
                dn(then, z).start()

        def extra_up():
            when(z == 0, lambda: yrecv_desc(a, z, 1).wait_recv())
            when(z > 0, lambda: extra(a, 0).wait_recv())
            extra(a, 0).start()
            if then is not None:
                up(then, z).start()

        when(jnp.logical_and(z == Z - s, z > 0), extra_dn)
        when(jnp.logical_and(z == s - 1, z < last), extra_up)

    def wait_y(a, zb):
        yrecv_desc(a, zb, 0).wait_recv()
        inner = jnp.logical_and(zb > 0, zb < last)
        when(inner, lambda: yrecv_desc(a, zb, 1).wait_recv())
        when(jnp.logical_and(zb == last, z == 0), lambda: extra(a, 1).wait_recv())
        when(jnp.logical_and(zb == 0, z == last), lambda: extra(a, 0).wait_recv())

    def at_distance(s, fn):
        when(z - s >= 0, lambda: fn(z - s))
        when(jnp.logical_and(s > 0, z + s <= last), lambda: fn(z + s))

    def by_distance(fn, far_first=False):
        loop(Z, lambda i: at_distance(last - i if far_first else i, fn))

    def sub_rows(ref, db):
        off = pl.multiple_of(lax.rem(db, q) * cols, cols)
        return ref.at[lax.div(db, q), pl.ds(off, cols), :]

    def mp_copy(a, buf, src, k, to):
        return send(buf.at[src], buf.at[src], as_.at[a, k], ar.at[a, src], (d, to))

    def mp_first(a, buf, op):
        for k in range(1, X):
            op(mp_copy(a, buf, m, X + k, lax.rem(chip + k, X) * 2 + core))
        op(mp_copy(a, buf, m, 0, partner))

    def mp_relay(a, buf):
        for k in range(1, X):
            src = lax.rem(chip + k, X) * 2 + core
            mp_copy(a, buf, src, k, partner).wait_recv()
            mp_copy(a, buf, src, k, partner).start()

    def mp_wait(a, buf):
        for k in range(X):
            src = lax.rem(chip + k, X) * 2 + 1 - core
            mp_copy(a, buf, src, k, partner).wait_recv()

    def mp_sent(a, buf):
        mp_first(a, buf, lambda c: c.wait_send())
        for k in range(1, X):
            mp_copy(a, buf, lax.rem(chip + k, X) * 2 + core, k, partner).wait_send()

    load[0].wait()
    for a in range(2):
        ag_own(a)
        y_sends(a, z, start)
    load[1].wait()
    mp_first(0, rbuf, start)
    for p in range(parts):
        load[6 + p].wait()

    def r_send(db):
        to, sub = lax.div(db, q), lax.rem(db, q)
        return send(ssend.at[db], rrecv.at[m, sub], rs.at[db], rr.at[m, sub], (d, to))

    def r_term(db):
        def one(t):
            term = lax.dot_general(
                gbuf[db, :, t], gbuf[d], (((0,), (0,)), ((), ())), preferred_element_type=f32
            )
            ssend[db, t, :] = term.astype(bf16)
        tiles(cols, min(256, cols), one)
        when(lax.div(db, q) != m, lambda: r_send(db).start())

    def rr_term(db):
        rhs = sub_rows(rbuf, db)
        def one(t):
            acc[t, :] += jnp.dot(gbuf[db, t, :], rhs[...], preferred_element_type=f32)
        tiles(rows, tile, one)

    def zero_acc():
        def one(t):
            acc[t, :] = jnp.zeros((tile, cols), f32)
        tiles(rows, tile, one)

    r_term(d)

    def g_step(i):
        s = i + 1
        ag_step(0, s)
        ag_step(1, s, then=2)
        when(s == min(2, last), lambda: mp_relay(0, rbuf))
        at_distance(s, lambda zb: r_term(zb * 2 + y))
    loop(Z - 1, g_step)
    y_sends(2, z, start)
    zero_acc()
    mp_wait(0, rbuf)
    by_distance(lambda zb: rr_term(zb * 2 + y))

    def y_block(zb):
        wait_y(0, zb)
        wait_y(1, zb)
        rr_term(zb * 2 + 1 - y)
    by_distance(y_block)

    def rr_out(t):
        rrbuf[m, t, :] = acc[t, :].astype(bf16)
    tiles(rows, tile, rr_out)
    mp_first(1, rrbuf, start)
    zero_acc()

    owner = lax.div(d, q)
    own_chip = lax.div(owner, 2)
    hd = dp // 2
    pair_off = pl.multiple_of(lax.rem(d, q) * cols, cols)

    def p_send(hb, i, to):
        view_p = pbuf.at[pl.ds(hb * hd, hd)]
        return send(view_p, view_p, ps.at[i], pr.at[hb], (d, to))

    def to_chips(op):
        for k in range(1, X):
            op(p_send(core, 2 + k, lax.rem(chip + k, X) * 2 + core))

    def own_pair():
        def copy(i):
            pbuf[i] = gbuf[i, pl.ds(pair_off, cols), :]
        loop(dp, copy)
        for hb in range(2):
            p_send(hb, hb, partner).start()
        to_chips(start)

    def near_pair():
        for hb in range(2):
            p_send(hb, hb, partner).wait_recv()
        to_chips(start)

    def far_pair():
        p_send(core, 0, partner).wait_recv()
        p_send(core, 0, partner).start()
        p_send(1 - core, 0, partner).wait_recv()

    when(m == owner, own_pair)

    def back_term(db, piece, t):
        _, c0, cw = piece
        off = pl.multiple_of(lax.rem(db, q) * cols + c0, cw)
        rhs = rbuf[lax.div(db, q), pl.ds(off, cw), :]
        return lax.dot_general(
            dbuf[t, :], rhs, (((1,), (1,)), ((), ())), preferred_element_type=f32
        )

    def by_send(i, piece, zb):
        p, c0, cw = piece
        c = pl.ds(c0, cw)
        return send(ysrc.at[zb, :, c], yrecv.at[p, zb, :, c], bys.at[i, zb], byr.at[i, zb], (ynbr, m))

    def rows_of(t, p):
        return pl.ds(pl.multiple_of(t.start + p * part, tile), tile)

    def scatter_first(p):
        for i, piece in enumerate(pieces[p], first_piece[p]):
            c = pl.ds(piece[1], piece[2])

            def one_block(zb, i=i, piece=piece, c=c):
                def one(t):
                    ysrc[zb, t, c] = back_term(zb * 2 + 1 - y, piece, rows_of(t, p)).astype(bf16)
                tiles(part, tile, one)
                by_send(i, piece, zb).start()
            by_distance(one_block, far_first=True)

    def bz_up(i, piece, zb):
        p, c0, cw = piece
        c = pl.ds(c0, cw)
        return send(yrecv.at[p, zb, :, c], zrecv.at[p, zb, :, c], bzs.at[i, zb], bzr.at[i, zb], (d + 2, m))

    def bz_dn(i, piece, zb):
        p, c0, cw = piece
        c = pl.ds(c0, cw)
        slot = jnp.where(zb == z - 1, Z, zb)
        return send(yrecv.at[p, zb, :, c], zrecv.at[p, slot, :, c], bzs.at[i, zb], bzr.at[i, slot], (d - 2, m))

    def line(i, piece, zb):
        p, c0, cw = piece
        c = pl.ds(c0, cw)
        by_send(i, piece, zb).wait_recv()

        def one(t):
            acc[t, pl.ds(0, cw)] = back_term(zb * 2 + y, piece, rows_of(t, p)) + yrecv[p, zb, t, c].astype(f32)
        tiles(part, tile, one)

        def add(slot):
            dst = zrecv.at[p, slot, :, c]
            send(dst, dst, bzs.at[i, 0], bzr.at[i, slot], (ynbr, m)).wait_recv()

            def more(t):
                acc[t, pl.ds(0, cw)] += zrecv[p, slot, t, c].astype(f32)
            tiles(part, tile, more)
        when(jnp.logical_and(zb >= z, z > 0), lambda: add(zb))
        when(jnp.logical_and(zb < z, z < last), lambda: add(zb))
        when(jnp.logical_and(zb == z, z < last), lambda: add(Z))

        def pack(t):
            yrecv[p, zb, t, c] = acc[t, pl.ds(0, cw)].astype(bf16)

        def keep(t):
            bbuf[rows_of(t, p), c] = acc[t, pl.ds(0, cw)].astype(bf16)
        when(zb != z, lambda: tiles(part, tile, pack))
        when(zb > z, lambda: bz_up(i, piece, zb).start())
        when(zb < z, lambda: bz_dn(i, piece, zb).start())
        when(zb == z, lambda: tiles(part, tile, keep))

    def scatter_step(p, s):
        for i, piece in enumerate(pieces[p], first_piece[p]):
            at_distance(s, lambda zb, i=i, piece=piece: line(i, piece, zb))

    def y_scattered(p):
        for i, piece in enumerate(pieces[p], first_piece[p]):
            loop(Z, lambda zb, i=i, piece=piece: by_send(i, piece, zb).wait_send())

    mom_tile = min(128, part)

    def m_term(p, db):
        rhs = sub_rows(rrbuf, db)
        def one(t):
            acc[t, :] += lax.dot_general(
                lbuf[p, db, :, t], rhs[...], (((0,), (0,)), ((), ())), preferred_element_type=f32
            )
        tiles(part, tile, one)

    def zero_part():
        def one(t):
            acc[t, :] = jnp.zeros((tile, cols), f32)
        tiles(part, tile, one)

    def moments(p):
        def one(t):
            w = pl.ds(pl.multiple_of(t.start + p * part, mom_tile), mom_tile)
            rot = acc[t, :]
            new1 = decay_moment * mom1[w, :] + (1.0 - decay_moment) * rot
            new2 = decay_moment * mom2[w, :] + (1.0 - decay_moment) * rot * rot
            mom1[w, :] = new1
            mom2[w, :] = new2
            dbuf[w, :] = (new1 / (jnp.sqrt(new2) + epsilon)).astype(bf16)
        tiles(part, mom_tile, one)

    def direction(p):
        def y_part(zb):
            wait_y(2 + p, zb)
            m_term(p, zb * 2 + 1 - y)
        by_distance(y_part)
        moments(p)

    by_distance(lambda zb: r_term(zb * 2 + 1 - y))

    def l_step(i):
        s = i + 1
        when(s == last, lambda: mp_relay(1, rrbuf))
        ag_step(2, s, then=3 if parts > 1 else None)
        when(jnp.logical_and(s == min(2, last), jnp.logical_and(chip == own_chip, m != owner)), near_pair)
    loop(Z - 1, l_step)
    if parts > 1:
        y_sends(3, z, start)
    mp_wait(1, rrbuf)
    load[2].wait()
    load[3].wait()
    by_distance(lambda zb: m_term(0, zb * 2 + y))
    direction(0)
    scatter_first(0)
    for p in range(1, parts):
        def both(i, p=p):
            s = i + 1
            ag_step(2 + p, s, then=3 + p if p + 1 < parts else None)
            scatter_step(p - 1, Z - s)
        loop(Z - 1, both)
        if p + 1 < parts:
            y_sends(3 + p, z, start)
        scatter_step(p - 1, 0)
        zero_part()
        by_distance(lambda zb, p=p: m_term(p, zb * 2 + y))
        direction(p)
        y_scattered(p - 1)
        scatter_first(p)

    stores = [
        pltpu.make_async_copy(a, b, store_sem.at[i])
        for i, (a, b) in enumerate([
            (mom1, out_first), (mom2, out_second), (fac_l, out_left), (fac_r, out_right), (dbuf, out_update)
        ])
    ]
    stores[0].start()
    stores[1].start()

    when(chip != own_chip, far_pair)
    load[4].wait()
    load[5].wait()

    for k in range(1, mp):
        src = lax.rem(m + k, mp)
        for sub in range(q):
            send(ssend.at[sub], rrecv.at[src, sub], rs.at[sub], rr.at[src, sub], (d, src)).wait_recv()
    for sub in range(q):
        def r_one(t, sub=sub):
            total = ssend[m * q + sub, t, :].astype(f32)
            for k in range(1, mp):
                total += rrecv[lax.rem(m + k, mp), sub, t, :].astype(f32)
            where = pl.ds(pl.multiple_of(sub * cols + t.start, 128), 128)
            fac_r[where, :] = decay_factor * fac_r[where, :] + (1.0 - decay_factor) * total
        tiles(cols, 128, r_one)
    stores[3].start()

    def l_scale(t):
        fac_l[t, :] = decay_factor * fac_l[t, :]
    tiles(rows, tile, l_scale)

    def l_term(db):
        def one(t):
            fac_l[t, :] += (1.0 - decay_factor) * lax.dot_general(
                gbuf[db, t, :], pbuf[db], (((1,), (1,)), ((), ())), preferred_element_type=f32
            )
        tiles(rows, tile, one)
    loop(dp, l_term)
    stores[2].start()
    loop(dp, lambda db: when(lax.div(db, q) != m, lambda: r_send(db).wait_send()))

    def u_near(h, c, xb, sub):
        db = (xb * 2 + 1 - core) * q + sub
        return send(
            ssend.at[db, :, c], urecv.at[0, xb, sub, :, c], us1.at[h, xb, sub], ur1.at[h, xb, sub], (d, partner)
        )

    def u_far(h, c, xb, sub):
        db = (xb * 2 + core) * q + sub
        return send(
            ssend.at[db, :, c], urecv.at[1, chip, sub, :, c], us2.at[h, xb, sub], ur2.at[h, chip, sub],
            (d, xb * 2 + core),
        )

    def u_got(h, c, which, xb, sub):
        dst = urecv.at[which, xb, sub, :, c]
        sem = ur1 if which == 0 else ur2
        send(dst, dst, us1.at[h, 0, 0], sem.at[h, xb, sub], (d, partner)).wait_recv()

    def u_dot(db, c):
        total = None
        for p in range(parts):
            term = jnp.dot(lbuf[p, db], bbuf[pl.ds(p * part, part), c], preferred_element_type=f32)
            total = term if total is None else total + term
        return total

    def u_terms(h, c):
        def near(i):
            xb, sub = lax.rem(chip + 1 + lax.div(i, q), X), lax.rem(i, q)
            db = (xb * 2 + 1 - core) * q + sub
            ssend[db, :, c] = u_dot(db, c).astype(bf16)
            u_near(h, c, xb, sub).start()
        loop(X * q, near)

        def far(i):
            xb, sub = lax.rem(chip + 1 + lax.div(i, q), X), lax.rem(i, q)
            db = (xb * 2 + core) * q + sub
            mine = u_dot(db, c)
            u_got(h, c, 0, xb, sub)
            ssend[db, :, c] = (mine + urecv[0, xb, sub, :, c].astype(f32)).astype(bf16)
            when(xb != chip, lambda: u_far(h, c, xb, sub).start())
        loop(X * q, far)

    def u_final(h, c):
        for sub in range(q):
            for k in range(1, X):
                u_got(h, c, 1, lax.rem(chip + k, X), sub)

            def one(t, sub=sub):
                total = ssend[m * q + sub, t, c].astype(f32)
                for k in range(1, X):
                    total += urecv[1, lax.rem(chip + k, X), sub, t, c].astype(f32)
                where = pl.ds(pl.multiple_of(sub * cols + t.start, 128), 128)
                bout[where, c] = total.astype(bf16)
            tiles(cols, 128, one)

    bout = dbuf
    p = parts - 1
    for h, piece in enumerate(pieces[p]):
        c = pl.ds(piece[1], piece[2])
        i = first_piece[p] + h
        by_distance(lambda zb, i=i, piece=piece: line(i, piece, zb), far_first=True)
        u_terms(h, c)
    for h, piece in enumerate(pieces[p]):
        u_final(h, pl.ds(piece[1], piece[2]))
    stores[4].start()

    for a in range(2 + parts):
        def sent(i, a=a):
            when(jnp.logical_and(z < last, i <= z), lambda: up(a, i).wait_send())
            when(jnp.logical_and(z > 0, i >= z), lambda: dn(a, i).wait_send())
            y_sends(a, i, lambda c: c.wait_send())
        loop(Z, sent)
        when(z > 0, lambda a=a: extra(a, 1).wait_send())
        when(z < last, lambda a=a: extra(a, 0).wait_send())
    mp_sent(0, rbuf)
    mp_sent(1, rrbuf)

    def near_sent():
        to_chips(lambda c: c.wait_send())
    when(chip == own_chip, near_sent)

    def own_sent():
        for hb in range(2):
            p_send(hb, hb, partner).wait_send()
    when(m == owner, own_sent)
    when(chip != own_chip, lambda: p_send(core, 0, partner).wait_send())
    y_scattered(parts - 1)
    for p in range(parts):
        for i, piece in enumerate(pieces[p], first_piece[p]):
            loop(Z, lambda zb, i=i, piece=piece: when(zb != z, lambda: bz_up(i, piece, zb).wait_send()))
    for h, piece in enumerate(pieces[parts - 1]):
        c = pl.ds(piece[1], piece[2])
        for sub in range(q):
            for xb in range(X):
                u_near(h, c, xb, sub).wait_send()
                when(xb != chip, lambda h=h, c=c, xb=xb, sub=sub: u_far(h, c, xb, sub).wait_send())
    for c in stores:
        c.wait()


def solution(mesh):
    dp, mp = mesh.shape["dp"], mesh.shape["mp"]
    Z, X = dp // 2, mp // 2

    def per_device(*args):
        _, rows, cols = args[0].shape
        q = rows // cols
        parts = min(PARTS, rows // 128)
        last_chunks = min(LAST, cols // 128)
        part, pieces = rows // parts, parts - 1 + last_chunks
        flat = [a.reshape(a.shape[1:]) for a in args]
        dma = pltpu.SemaphoreType.DMA
        outs = pl.pallas_call(
            functools.partial(kernel, dp, mp, rows, cols, parts, last_chunks),
            out_shape=[jax.ShapeDtypeStruct((rows, cols), t) for t in (f32, f32, f32, f32, bf16)],
            in_specs=[pl.BlockSpec(memory_space=pl.ANY)] * 7,
            out_specs=[pl.BlockSpec(memory_space=pl.ANY)] * 5,
            scratch_shapes=[
                pltpu.VMEM((dp, rows, cols), bf16),
                pltpu.VMEM((parts, dp, cols, part), bf16),
                pltpu.VMEM((mp, rows, cols), bf16),
                pltpu.VMEM((mp, rows, cols), bf16),
                pltpu.VMEM((dp, cols, cols), bf16),
                pltpu.VMEM((dp, cols, cols), bf16),
                pltpu.VMEM((mp, q, cols, cols), bf16),
                pltpu.VMEM((2, X, q, cols, cols), bf16),
                pltpu.VMEM((Z, part, cols), bf16),
                pltpu.VMEM((parts, Z, part, cols), bf16),
                pltpu.VMEM((parts, Z + 1, part, cols), bf16),
                pltpu.VMEM((rows, cols), f32),
                pltpu.VMEM((rows, cols), f32),
                pltpu.VMEM((rows, cols), f32),
                pltpu.VMEM((rows, cols), f32),
                pltpu.VMEM((rows, cols), f32),
                pltpu.VMEM((rows, cols), bf16),
                pltpu.VMEM((rows, cols), bf16),
                dma((6 + parts,)),
                dma((5,)),
                dma((2 + parts, Z)),
                dma((2 + parts, Z)),
                dma((2 + parts, Z)),
                dma((2 + parts, Z, 2)),
                dma((2 + parts, Z, 2)),
                dma((2 + parts, 2)),
                dma((2 + parts, 2)),
                dma((2, 2 * X)),
                dma((2, mp)),
                dma((dp,)),
                dma((mp, q)),
                dma((last_chunks, X, q)),
                dma((last_chunks, X, q)),
                dma((last_chunks, X, q)),
                dma((last_chunks, X, q)),
                dma((2 + X,)),
                dma((2,)),
                dma((pieces, Z)),
                dma((pieces, Z)),
                dma((pieces, Z)),
                dma((pieces, Z + 1)),
            ],
            compiler_params=pltpu.CompilerParams(
                collective_id=0, has_side_effects=True, vmem_limit_bytes=67043328
            ),
        )(*flat)
        return tuple(o.reshape((1,) + o.shape) for o in outs)

    return jax.shard_map(
        per_device,
        mesh=mesh,
        in_specs=(P(None, "mp", "dp"),) * 5 + (P(None, "dp", "mp"), P(None, "mp", "dp")),
        out_specs=(P(None, "mp", "dp"),) * 5,
        check_vma=False,
    )
```

time: 329 us -> 329 us (level); the launches traced: 328 us -> 323 us
  Pallas kernels: 317 us -> 311 us
    pallas_call x1, Pallas kernels: 317 us -> 311 us  [per_device(): pl.pallas_call(functools.partial(kernel, dp, mp, rows, cols, parts, last_...]
where the time goes in v1:
time: 329 us; the launch traced here: 323 us
  Pallas kernels  311 us (95%)
  local copies, waits for them, and re-layouts  10.9 us (3%)
    pallas_call x1, Pallas kernels, per_device(): pl.pallas_call(functools.partial(kernel, dp, mp, rows, cols, parts, last_...  311 us
    unnamed x13, local copies, waits for them, and re-layouts  10.9 us

profile of v1, /device:TPU:12, one launch (start us, length us, event | category | flops | bytes accessed | tf_op | source)
XLA Modules:
  0.0 322.6 jit_solution(10536965083444062339)
XLA Ops:
  0.6 311.1 %shard_map.110 = (f32[1024,512]{1,0:T(8,128)}, f32[1024,512]{1,0:T(8,128)}, f32[1024,512]{1,0:T(8,128)}, f32[1024,512]{1,0:T(8,128)}, bf16[1024,512]{1,0:T(8,128)(2,1)}) custom-call(bf16[1024,512]{1,0:T(8,128)(2,1)} %bitcast.21, f32[1024,512]{1,0:T(8,128)} %bitcast.16, f32[1024,512]{1,0:T(8,128)} %bitcast.17, f32[1024,512]{1,0:T(8,128)} %bitcast.18, ...), custom_call_target="tpu_custom_call" | custom-call | tf_op jit(solution)/shard_map/pallas_call | solution.py:581
  311.7 0.0 copy-start.2
  311.7 3.2 %copy.17 = f32[1,1024,512]{2,1,0:T(8,128)} copy(f32[1,1024,512]{2,1,0:T(8,128)} %bitcast.15) | data formatting | bytes 4194304
  315.0 0.0 copy-done.2
  315.0 0.0 copy-start.1
  315.0 1.3 copy.18
  316.3 1.0 copy-done.1
  317.3 0.0 copy-start
  317.3 1.3 copy.19
  318.6 1.0 copy-done
  319.7 0.0 copy-start.3
  319.7 1.3 copy.20
  321.0 0.6 copy-done.3
  321.6 1.0 copy.21
Async XLA Ops:
  311.7 3.2 %copy-start.2 = (f32[1024,512]{1,0:T(8,128)S(1)}, f32[1024,512]{1,0:T(8,128)}, u32[]{:S(2)}) copy-start(f32[1024,512]{1,0:T(8,128)} %get-tuple-element.11) | copy-start | bytes 6291460
  315.0 2.3 copy-start.1
  317.3 2.3 copy-start
  319.7 2.0 copy-start.3

commit v2 on v1

--- a/solution.py
+++ b/solution.py
@@ -13,17 +13,36 @@
 bf16, f32 = jnp.bfloat16, jnp.float32
 MESH = pl.DeviceIdType.MESH
 PARTS, LAST = 2, 4
+Y_FIRST, Z_FIRST = 0, 1
+
+
+def scatter_pieces(rows, cols, parts, last_chunks):
+    part = rows // parts
+    out = [[] for _ in range(parts)]
+    for p in range(parts - 1):
+        out[p].append((p, 0, part // 2, 0, cols, Z_FIRST))
+        out[p].append((p, part // 2, part // 2, 0, cols, Y_FIRST))
+    for h in range(last_chunks):
+        cw = cols // last_chunks
+        out[parts - 1].append((parts - 1, 0, part, h * cw, cw, Y_FIRST))
+    return out
 
 
 def kernel(dp, mp, rows, cols, parts, last_chunks, *refs):
+    pieces = scatter_pieces(rows, cols, parts, last_chunks)
+    first_piece = [sum(len(x) for x in pieces[:p]) for p in range(parts)]
+    n_pieces = sum(len(x) for x in pieces)
     (grad, first, second, left_f, right_f, left_b, right_b,
      out_first, out_second, out_left, out_right, out_update,
-     gbuf, lbuf, rbuf, rrbuf, pbuf, ssend, rrecv, urecv, ysrc, yrecv, zrecv,
-     fac_l, fac_r, mom1, mom2, acc, dbuf, bbuf,
+     gbuf, lbuf, rbuf, rrbuf, pbuf, ssend, r1buf, r2buf, u1buf, u2buf,
+     fac, mom1, mom2, acc, dbuf, bbuf,
      load_sem, store_sem, zs_up, zs_dn, zr, ys, yr, es, er, as_, ar,
-     rs, rr, us1, ur1, us2, ur2, ps, pr, bys, byr, bzs, bzr) = refs
+     rs1, rr1, rs2, rr2, us1, ur1, us2, ur2, ps, pr, bys, byr, bzs, bzr) = refs[:53]
+    out_bufs = refs[53:53 + n_pieces]
+    y_bufs = refs[53 + n_pieces:53 + 2 * n_pieces]
+    z_bufs = refs[53 + 2 * n_pieces:]
     Z, q, X = dp // 2, rows // cols, mp // 2
-    part = rows // parts
+    part, cw = rows // parts, cols // last_chunks
     d, m = lax.axis_index("dp"), lax.axis_index("mp")
     z, y = lax.div(d, 2), lax.rem(d, 2)
     core, chip = lax.rem(m, 2), lax.div(m, 2)
@@ -31,11 +50,6 @@
     last = Z - 1
     ynbr = z * 2 + (1 - y)
     tile = min(256, part)
-    pieces = []
-    for p in range(parts):
-        n = last_chunks if p == parts - 1 else 1
-        pieces.append([(p, i * (cols // n), cols // n) for i in range(n)])
-    first_piece = [sum(len(x) for x in pieces[:p]) for p in range(parts)]
 
     def send(src, dst, s, r, dev):
         return pltpu.make_async_remote_copy(
@@ -55,12 +69,34 @@
         loop(n // size, lambda i: fn(pl.ds(pl.multiple_of(base + i * size, size), size)))
 
     loads = [
-        (grad, gbuf.at[d]), (right_b, rbuf.at[m]),
-        (first, mom1), (second, mom2), (left_f, fac_l), (right_f, fac_r),
+        (grad, gbuf.at[d]), (right_b, rbuf.at[m]), (right_f, fac),
     ]
     loads += [(left_b.at[:, pl.ds(p * part, part)], lbuf.at[p, d]) for p in range(parts)]
     load = [pltpu.make_async_copy(a, b, load_sem.at[i]) for i, (a, b) in enumerate(loads)]
     for c in load:
+        c.start()
+
+    def part_rows(ref, p):
+        return ref.at[pl.ds(p * part, part), :]
+
+    def mom_loads(p):
+        n = 4 + parts + 2 * p
+        return [
+            pltpu.make_async_copy(part_rows(a, p), b, load_sem.at[n + i])
+            for i, (a, b) in enumerate([(first, mom1), (second, mom2)])
+        ]
+
+    def mom_stores(p):
+        return [
+            pltpu.make_async_copy(b, part_rows(a, p), store_sem.at[3 + 2 * p + i])
+            for i, (a, b) in enumerate([(out_first, mom1), (out_second, mom2)])
+        ]
+
+    load_left = pltpu.make_async_copy(left_f, fac, load_sem.at[3 + parts])
+    store_right = pltpu.make_async_copy(fac, out_right, store_sem.at[0])
+    store_left = pltpu.make_async_copy(fac, out_left, store_sem.at[1])
+    store_update = pltpu.make_async_copy(dbuf, out_update, store_sem.at[2])
+    for c in mom_loads(0):
         c.start()
 
     barrier = pltpu.get_barrier_semaphore()
@@ -200,20 +236,40 @@
     load[1].wait()
     mp_first(0, rbuf, start)
     for p in range(parts):
-        load[6 + p].wait()
-
-    def r_send(db):
-        to, sub = lax.div(db, q), lax.rem(db, q)
-        return send(ssend.at[db], rrecv.at[m, sub], rs.at[db], rr.at[m, sub], (d, to))
+        load[3 + p].wait()
+
+    def far_slot(k):
+        return lax.rem(k + X, X) - 1
+
+    def r_near(db):
+        xb, sub = lax.div(db, 2 * q), lax.rem(db, q)
+        return send(ssend.at[:, db], r1buf.at[:, xb, sub], rs1.at[xb, sub], rr1.at[xb, sub], (d, partner))
+
+    def r_far(db):
+        xb, sub = lax.div(db, 2 * q), lax.rem(db, q)
+        slot = far_slot(chip - xb)
+        return send(ssend.at[:, db], r2buf.at[:, slot, sub], rs2.at[xb, sub], rr2.at[slot, sub], (d, xb * 2 + core))
 
     def r_term(db):
+        xb, sub = lax.div(db, 2 * q), lax.rem(db, q)
+        mine = lax.rem(lax.div(db, q), 2) == core
+
         def one(t):
             term = lax.dot_general(
                 gbuf[db, :, t], gbuf[d], (((0,), (0,)), ((), ())), preferred_element_type=f32
             )
-            ssend[db, t, :] = term.astype(bf16)
+            for h in range(last_chunks):
+                ssend[h, db, t, :] = term[:, h * cw:(h + 1) * cw].astype(bf16)
         tiles(cols, min(256, cols), one)
-        when(lax.div(db, q) != m, lambda: r_send(db).start())
+
+        def add():
+            got = r1buf.at[:, xb, sub]
+            send(got, got, rs1.at[0, 0], rr1.at[xb, sub], (d, partner)).wait_recv()
+            for h in range(last_chunks):
+                ssend[h, db] = (ssend[h, db].astype(f32) + r1buf[h, xb, sub].astype(f32)).astype(bf16)
+            when(xb != chip, lambda: r_far(db).start())
+        when(jnp.logical_not(mine), lambda: r_near(db).start())
+        when(mine, add)
 
     def rr_term(db):
         rhs = sub_rows(rbuf, db)
@@ -286,80 +342,117 @@
     when(m == owner, own_pair)
 
     def back_term(db, piece, t):
-        _, c0, cw = piece
-        off = pl.multiple_of(lax.rem(db, q) * cols + c0, cw)
-        rhs = rbuf[lax.div(db, q), pl.ds(off, cw), :]
+        p, r0, _, c0, w, _ = piece
+        off = pl.multiple_of(lax.rem(db, q) * cols + c0, w)
+        rhs = rbuf[lax.div(db, q), pl.ds(off, w), :]
+        mine = pl.ds(pl.multiple_of(t.start + (p * part + r0), t.size), t.size)
         return lax.dot_general(
-            dbuf[t, :], rhs, (((1,), (1,)), ((), ())), preferred_element_type=f32
+            dbuf[mine, :], rhs, (((1,), (1,)), ((), ())), preferred_element_type=f32
         )
 
-    def by_send(i, piece, zb):
-        p, c0, cw = piece
-        c = pl.ds(c0, cw)
-        return send(ysrc.at[zb, :, c], yrecv.at[p, zb, :, c], bys.at[i, zb], byr.at[i, zb], (ynbr, m))
-
-    def rows_of(t, p):
-        return pl.ds(pl.multiple_of(t.start + p * part, tile), tile)
+    def piece_tiles(piece, fn):
+        tiles(piece[2], min(256, piece[2]), fn)
+
+    def by_send(i, zb):
+        return send(out_bufs[i].at[zb], y_bufs[i].at[zb], bys.at[i, zb], byr.at[i, zb], (ynbr, m))
+
+    def by_last(i):
+        return send(out_bufs[i].at[z, 1 - y], y_bufs[i], bys.at[i, 0], byr.at[i, 0], (ynbr, m))
+
+    def bz_up(i, zb, src):
+        return send(src.at[zb], z_bufs[i].at[zb], bzs.at[i, zb], bzr.at[i, zb], (d + 2, m))
+
+    def bz_dn(i, zb, src):
+        slot = jnp.where(zb == z - 1, Z, zb)
+        return send(src.at[zb], z_bufs[i].at[slot], bzs.at[i, zb], bzr.at[i, slot], (d - 2, m))
+
+    def z_arrivals(i, zb, add):
+        def one(slot):
+            dst = z_bufs[i].at[slot]
+            send(dst, dst, bzs.at[i, 0], bzr.at[i, slot], (ynbr, m)).wait_recv()
+            add(slot)
+        when(jnp.logical_and(zb >= z, z > 0), lambda: one(zb))
+        when(jnp.logical_and(zb < z, z < last), lambda: one(zb))
+        when(jnp.logical_and(zb == z, z < last), lambda: one(Z))
+
+    def z_send(i, zb, src):
+        when(zb > z, lambda: bz_up(i, zb, src).start())
+        when(zb < z, lambda: bz_dn(i, zb, src).start())
+
+    def to_back(piece, t, value):
+        p, r0, _, c0, w, _ = piece
+        mine = pl.ds(pl.multiple_of(t.start + (p * part + r0), t.size), t.size)
+        bbuf[mine, pl.ds(c0, w)] = value.astype(bf16)
+
+    def line_y_first(i, piece, zb):
+        c = pl.ds(0, piece[4])
+        by_send(i, zb).wait_recv()
+
+        def one(t):
+            acc[t, c] = back_term(zb * 2 + y, piece, t) + y_bufs[i][zb, t, :].astype(f32)
+        piece_tiles(piece, one)
+
+        def add(slot):
+            def more(t):
+                acc[t, c] += z_bufs[i][slot, t, :].astype(f32)
+            piece_tiles(piece, more)
+        z_arrivals(i, zb, add)
+
+        def pack(t):
+            y_bufs[i][zb, t, :] = acc[t, c].astype(bf16)
+        when(zb != z, lambda: piece_tiles(piece, pack))
+        z_send(i, zb, y_bufs[i])
+        when(zb == z, lambda: piece_tiles(piece, lambda t: to_back(piece, t, acc[t, c])))
+
+    def line_z_first(i, piece, zb):
+        n = piece[2]
+
+        def rows_of(t, yy):
+            return pl.ds(pl.multiple_of(t.start + yy * n, t.size), t.size)
+        for yy in range(2):
+            def one(t, yy=yy):
+                acc[rows_of(t, yy), :] = back_term(zb * 2 + yy, piece, t)
+            piece_tiles(piece, one)
+
+        def add(slot):
+            for yy in range(2):
+                def more(t, yy=yy):
+                    acc[rows_of(t, yy), :] += z_bufs[i][slot, yy, t, :].astype(f32)
+                piece_tiles(piece, more)
+        z_arrivals(i, zb, add)
+        for yy in range(2):
+            def pack(t, yy=yy):
+                out_bufs[i][zb, yy, t, :] = acc[rows_of(t, yy), :].astype(bf16)
+            piece_tiles(piece, pack)
+        z_send(i, zb, out_bufs[i])
+        when(zb == z, lambda: by_last(i).start())
+
+    def finish_z_first(i, piece):
+        by_last(i).wait_recv()
+
+        def one(t):
+            mine = out_bufs[i][z, y, t, :].astype(f32) + y_bufs[i][t, :].astype(f32)
+            to_back(piece, t, mine)
+        piece_tiles(piece, one)
+
+    def numbered(p):
+        return list(enumerate(pieces[p], first_piece[p]))
 
     def scatter_first(p):
-        for i, piece in enumerate(pieces[p], first_piece[p]):
-            c = pl.ds(piece[1], piece[2])
-
-            def one_block(zb, i=i, piece=piece, c=c):
+        for i, piece in numbered(p):
+            if piece[5] == Z_FIRST:
+                continue
+
+            def one_block(zb, i=i, piece=piece):
                 def one(t):
-                    ysrc[zb, t, c] = back_term(zb * 2 + 1 - y, piece, rows_of(t, p)).astype(bf16)
-                tiles(part, tile, one)
-                by_send(i, piece, zb).start()
+                    out_bufs[i][zb, t, :] = back_term(zb * 2 + 1 - y, piece, t).astype(bf16)
+                piece_tiles(piece, one)
+                by_send(i, zb).start()
             by_distance(one_block, far_first=True)
 
-    def bz_up(i, piece, zb):
-        p, c0, cw = piece
-        c = pl.ds(c0, cw)
-        return send(yrecv.at[p, zb, :, c], zrecv.at[p, zb, :, c], bzs.at[i, zb], bzr.at[i, zb], (d + 2, m))
-
-    def bz_dn(i, piece, zb):
-        p, c0, cw = piece
-        c = pl.ds(c0, cw)
-        slot = jnp.where(zb == z - 1, Z, zb)
-        return send(yrecv.at[p, zb, :, c], zrecv.at[p, slot, :, c], bzs.at[i, zb], bzr.at[i, slot], (d - 2, m))
-
-    def line(i, piece, zb):
-        p, c0, cw = piece
-        c = pl.ds(c0, cw)
-        by_send(i, piece, zb).wait_recv()
-
-        def one(t):
-            acc[t, pl.ds(0, cw)] = back_term(zb * 2 + y, piece, rows_of(t, p)) + yrecv[p, zb, t, c].astype(f32)
-        tiles(part, tile, one)
-
-        def add(slot):
-            dst = zrecv.at[p, slot, :, c]
-            send(dst, dst, bzs.at[i, 0], bzr.at[i, slot], (ynbr, m)).wait_recv()
-
-            def more(t):
-                acc[t, pl.ds(0, cw)] += zrecv[p, slot, t, c].astype(f32)
-            tiles(part, tile, more)
-        when(jnp.logical_and(zb >= z, z > 0), lambda: add(zb))
-        when(jnp.logical_and(zb < z, z < last), lambda: add(zb))
-        when(jnp.logical_and(zb == z, z < last), lambda: add(Z))
-
-        def pack(t):
-            yrecv[p, zb, t, c] = acc[t, pl.ds(0, cw)].astype(bf16)
-
-        def keep(t):
-            bbuf[rows_of(t, p), c] = acc[t, pl.ds(0, cw)].astype(bf16)
-        when(zb != z, lambda: tiles(part, tile, pack))
-        when(zb > z, lambda: bz_up(i, piece, zb).start())
-        when(zb < z, lambda: bz_dn(i, piece, zb).start())
-        when(zb == z, lambda: tiles(part, tile, keep))
-
-    def scatter_step(p, s):
-        for i, piece in enumerate(pieces[p], first_piece[p]):
-            at_distance(s, lambda zb, i=i, piece=piece: line(i, piece, zb))
-
-    def y_scattered(p):
-        for i, piece in enumerate(pieces[p], first_piece[p]):
-            loop(Z, lambda zb, i=i, piece=piece: by_send(i, piece, zb).wait_send())
+    def scatter_step(i, piece, s):
+        fn = line_z_first if piece[5] == Z_FIRST else line_y_first
+        at_distance(s, lambda zb: fn(i, piece, zb))
 
     mom_tile = min(128, part)
 
@@ -380,10 +473,10 @@
         def one(t):
             w = pl.ds(pl.multiple_of(t.start + p * part, mom_tile), mom_tile)
             rot = acc[t, :]
-            new1 = decay_moment * mom1[w, :] + (1.0 - decay_moment) * rot
-            new2 = decay_moment * mom2[w, :] + (1.0 - decay_moment) * rot * rot
-            mom1[w, :] = new1
-            mom2[w, :] = new2
+            new1 = decay_moment * mom1[t, :] + (1.0 - decay_moment) * rot
+            new2 = decay_moment * mom2[t, :] + (1.0 - decay_moment) * rot * rot
+            mom1[t, :] = new1
+            mom2[t, :] = new2
             dbuf[w, :] = (new1 / (jnp.sqrt(new2) + epsilon)).astype(bf16)
         tiles(part, mom_tile, one)
 
@@ -392,7 +485,11 @@
             wait_y(2 + p, zb)
             m_term(p, zb * 2 + 1 - y)
         by_distance(y_part)
+        for c in mom_loads(p):
+            c.wait()
         moments(p)
+        for c in mom_stores(p):
+            c.start()
 
     by_distance(lambda zb: r_term(zb * 2 + 1 - y))
 
@@ -405,132 +502,145 @@
     if parts > 1:
         y_sends(3, z, start)
     mp_wait(1, rrbuf)
-    load[2].wait()
-    load[3].wait()
     by_distance(lambda zb: m_term(0, zb * 2 + y))
     direction(0)
     scatter_first(0)
+
+    def r_final():
+        for sub in range(q):
+            for k in range(1, X):
+                got = r2buf.at[:, k - 1, sub]
+                send(got, got, rs1.at[0, 0], rr2.at[k - 1, sub], (d, partner)).wait_recv()
+            for h in range(last_chunks):
+                def one(t, sub=sub, h=h):
+                    total = ssend[h, m * q + sub, t, :].astype(f32)
+                    for k in range(1, X):
+                        total += r2buf[h, k - 1, sub, t, :].astype(f32)
+                    where = pl.ds(pl.multiple_of(sub * cols + t.start, 128), 128)
+                    c = pl.ds(h * cw, cw)
+                    fac[where, c] = decay_factor * fac[where, c] + (1.0 - decay_factor) * total
+                tiles(cols, 128, one)
+    load[2].wait()
+    r_final()
+    store_right.start()
+
+    def l_term(db):
+        def one(t):
+            fac[t, :] += (1.0 - decay_factor) * lax.dot_general(
+                gbuf[db, t, :], pbuf[db], (((1,), (1,)), ((), ())), preferred_element_type=f32
+            )
+        tiles(rows, tile, one)
+
     for p in range(1, parts):
         def both(i, p=p):
             s = i + 1
             ag_step(2 + p, s, then=3 + p if p + 1 < parts else None)
-            scatter_step(p - 1, Z - s)
+            for j, piece in numbered(p - 1):
+                scatter_step(j, piece, Z - s)
         loop(Z - 1, both)
         if p + 1 < parts:
             y_sends(3 + p, z, start)
-        scatter_step(p - 1, 0)
+        for j, piece in numbered(p - 1):
+            scatter_step(j, piece, 0)
         zero_part()
+        for c in mom_stores(p - 1):
+            c.wait()
+        for c in mom_loads(p):
+            c.start()
+        if p == 1:
+            store_right.wait()
+            load_left.start()
         by_distance(lambda zb, p=p: m_term(p, zb * 2 + y))
         direction(p)
-        y_scattered(p - 1)
         scatter_first(p)
-
-    stores = [
-        pltpu.make_async_copy(a, b, store_sem.at[i])
-        for i, (a, b) in enumerate([
-            (mom1, out_first), (mom2, out_second), (fac_l, out_left), (fac_r, out_right), (dbuf, out_update)
-        ])
-    ]
-    stores[0].start()
-    stores[1].start()
+        for j, piece in numbered(p - 1):
+            if piece[5] == Z_FIRST:
+                finish_z_first(j, piece)
 
     when(chip != own_chip, far_pair)
-    load[4].wait()
-    load[5].wait()
-
-    for k in range(1, mp):
-        src = lax.rem(m + k, mp)
-        for sub in range(q):
-            send(ssend.at[sub], rrecv.at[src, sub], rs.at[sub], rr.at[src, sub], (d, src)).wait_recv()
-    for sub in range(q):
-        def r_one(t, sub=sub):
-            total = ssend[m * q + sub, t, :].astype(f32)
-            for k in range(1, mp):
-                total += rrecv[lax.rem(m + k, mp), sub, t, :].astype(f32)
-            where = pl.ds(pl.multiple_of(sub * cols + t.start, 128), 128)
-            fac_r[where, :] = decay_factor * fac_r[where, :] + (1.0 - decay_factor) * total
-        tiles(cols, 128, r_one)
-    stores[3].start()
+    load_left.wait()
 
     def l_scale(t):
-        fac_l[t, :] = decay_factor * fac_l[t, :]
+        fac[t, :] = decay_factor * fac[t, :]
     tiles(rows, tile, l_scale)
 
-    def l_term(db):
-        def one(t):
-            fac_l[t, :] += (1.0 - decay_factor) * lax.dot_general(
-                gbuf[db, t, :], pbuf[db], (((1,), (1,)), ((), ())), preferred_element_type=f32
-            )
-        tiles(rows, tile, one)
-    loop(dp, l_term)
-    stores[2].start()
-    loop(dp, lambda db: when(lax.div(db, q) != m, lambda: r_send(db).wait_send()))
-
-    def u_near(h, c, xb, sub):
+    def r_sent(db):
+        mine = lax.rem(lax.div(db, q), 2) == core
+        when(jnp.logical_not(mine), lambda: r_near(db).wait_send())
+        when(jnp.logical_and(mine, lax.div(db, 2 * q) != chip), lambda: r_far(db).wait_send())
+    loop(dp, r_sent)
+
+    def u_near(h, xb, sub):
         db = (xb * 2 + 1 - core) * q + sub
         return send(
-            ssend.at[db, :, c], urecv.at[0, xb, sub, :, c], us1.at[h, xb, sub], ur1.at[h, xb, sub], (d, partner)
+            ssend.at[h, db], u1buf.at[h, xb, sub], us1.at[h, xb, sub], ur1.at[h, xb, sub], (d, partner)
         )
 
-    def u_far(h, c, xb, sub):
+    def u_far(h, xb, sub):
         db = (xb * 2 + core) * q + sub
+        slot = far_slot(chip - xb)
         return send(
-            ssend.at[db, :, c], urecv.at[1, chip, sub, :, c], us2.at[h, xb, sub], ur2.at[h, chip, sub],
-            (d, xb * 2 + core),
+            ssend.at[h, db], u2buf.at[h, slot, sub], us2.at[h, xb, sub], ur2.at[h, slot, sub], (d, xb * 2 + core)
         )
 
-    def u_got(h, c, which, xb, sub):
-        dst = urecv.at[which, xb, sub, :, c]
-        sem = ur1 if which == 0 else ur2
-        send(dst, dst, us1.at[h, 0, 0], sem.at[h, xb, sub], (d, partner)).wait_recv()
-
-    def u_dot(db, c):
+    def u_got(dst, sem):
+        send(dst, dst, us1.at[0, 0, 0], sem, (d, partner)).wait_recv()
+
+    def u_dot(h, db):
+        c = pl.ds(h * cw, cw)
         total = None
         for p in range(parts):
             term = jnp.dot(lbuf[p, db], bbuf[pl.ds(p * part, part), c], preferred_element_type=f32)
             total = term if total is None else total + term
         return total
 
-    def u_terms(h, c):
+    def u_terms(h):
         def near(i):
             xb, sub = lax.rem(chip + 1 + lax.div(i, q), X), lax.rem(i, q)
             db = (xb * 2 + 1 - core) * q + sub
-            ssend[db, :, c] = u_dot(db, c).astype(bf16)
-            u_near(h, c, xb, sub).start()
+            ssend[h, db] = u_dot(h, db).astype(bf16)
+            u_near(h, xb, sub).start()
         loop(X * q, near)
 
         def far(i):
             xb, sub = lax.rem(chip + 1 + lax.div(i, q), X), lax.rem(i, q)
             db = (xb * 2 + core) * q + sub
-            mine = u_dot(db, c)
-            u_got(h, c, 0, xb, sub)
-            ssend[db, :, c] = (mine + urecv[0, xb, sub, :, c].astype(f32)).astype(bf16)
-            when(xb != chip, lambda: u_far(h, c, xb, sub).start())
+            mine = u_dot(h, db)
+            u_got(u1buf.at[h, xb, sub], ur1.at[h, xb, sub])
+            ssend[h, db] = (mine + u1buf[h, xb, sub].astype(f32)).astype(bf16)
+            when(xb != chip, lambda: u_far(h, xb, sub).start())
         loop(X * q, far)
 
-    def u_final(h, c):
+    def u_final(h):
+        c = pl.ds(h * cw, cw)
         for sub in range(q):
             for k in range(1, X):
-                u_got(h, c, 1, lax.rem(chip + k, X), sub)
+                u_got(u2buf.at[h, k - 1, sub], ur2.at[h, k - 1, sub])
 
             def one(t, sub=sub):
-                total = ssend[m * q + sub, t, c].astype(f32)
+                total = ssend[h, m * q + sub, t, :].astype(f32)
                 for k in range(1, X):
-                    total += urecv[1, lax.rem(chip + k, X), sub, t, c].astype(f32)
+                    total += u2buf[h, k - 1, sub, t, :].astype(f32)
                 where = pl.ds(pl.multiple_of(sub * cols + t.start, 128), 128)
-                bout[where, c] = total.astype(bf16)
+                dbuf[where, c] = total.astype(bf16)
             tiles(cols, 128, one)
 
-    bout = dbuf
-    p = parts - 1
-    for h, piece in enumerate(pieces[p]):
-        c = pl.ds(piece[1], piece[2])
-        i = first_piece[p] + h
-        by_distance(lambda zb, i=i, piece=piece: line(i, piece, zb), far_first=True)
-        u_terms(h, c)
-    for h, piece in enumerate(pieces[p]):
-        u_final(h, pl.ds(piece[1], piece[2]))
-    stores[4].start()
+    done = 0
+    for tau in range(last_chunks + Z - 1):
+        for h, (i, piece) in enumerate(numbered(parts - 1)):
+            if 0 <= tau - h <= last:
+                scatter_step(i, piece, last - (tau - h))
+                if tau - h == last:
+                    u_terms(h)
+        per = -(-dp // (last_chunks + Z - 2))
+        for db in range(done, min(done + per, dp)):
+            l_term(db)
+        done = min(done + per, dp)
+        if tau * per < dp <= (tau + 1) * per:
+            store_left.start()
+    for h in range(last_chunks):
+        u_final(h)
+    store_update.start()
 
     for a in range(2 + parts):
         def sent(i, a=a):
@@ -552,17 +662,25 @@
             p_send(hb, hb, partner).wait_send()
     when(m == owner, own_sent)
     when(chip != own_chip, lambda: p_send(core, 0, partner).wait_send())
-    y_scattered(parts - 1)
+    def line_sent(i, piece):
+        src = out_bufs[i] if piece[5] == Z_FIRST else y_bufs[i]
+
+        def one(zb):
+            if piece[5] == Y_FIRST:
+                by_send(i, zb).wait_send()
+            when(zb != z, lambda: bz_up(i, zb, src).wait_send())
+        loop(Z, one)
+        if piece[5] == Z_FIRST:
+            by_last(i).wait_send()
     for p in range(parts):
-        for i, piece in enumerate(pieces[p], first_piece[p]):
-            loop(Z, lambda zb, i=i, piece=piece: when(zb != z, lambda: bz_up(i, piece, zb).wait_send()))
-    for h, piece in enumerate(pieces[parts - 1]):
-        c = pl.ds(piece[1], piece[2])
+        for i, piece in numbered(p):
+            line_sent(i, piece)
+    for h in range(last_chunks):
         for sub in range(q):
             for xb in range(X):
-                u_near(h, c, xb, sub).wait_send()
-                when(xb != chip, lambda h=h, c=c, xb=xb, sub=sub: u_far(h, c, xb, sub).wait_send())
-    for c in stores:
+                u_near(h, xb, sub).wait_send()
+                when(xb != chip, lambda h=h, xb=xb, sub=sub: u_far(h, xb, sub).wait_send())
+    for c in mom_stores(parts - 1) + [store_left, store_update]:
         c.wait()
 
 
@@ -575,7 +693,15 @@
         q = rows // cols
         parts = min(PARTS, rows // 128)
         last_chunks = min(LAST, cols // 128)
-        part, pieces = rows // parts, parts - 1 + last_chunks
+        part, cw = rows // parts, cols // last_chunks
+        pieces = sum(scatter_pieces(rows, cols, parts, last_chunks), [])
+        n = len(pieces)
+        out_b, y_b, z_b = [], [], []
+        for _, _, nr, _, w, kind in pieces:
+            lead = (2,) if kind == Z_FIRST else ()
+            out_b.append(pltpu.VMEM((Z,) + lead + (nr, w), bf16))
+            y_b.append(pltpu.VMEM((nr, w) if lead else (Z, nr, w), bf16))
+            z_b.append(pltpu.VMEM((Z + 1,) + lead + (nr, w), bf16))
         flat = [a.reshape(a.shape[1:]) for a in args]
         dma = pltpu.SemaphoreType.DMA
         outs = pl.pallas_call(
@@ -589,21 +715,19 @@
                 pltpu.VMEM((mp, rows, cols), bf16),
                 pltpu.VMEM((mp, rows, cols), bf16),
                 pltpu.VMEM((dp, cols, cols), bf16),
-                pltpu.VMEM((dp, cols, cols), bf16),
-                pltpu.VMEM((mp, q, cols, cols), bf16),
-                pltpu.VMEM((2, X, q, cols, cols), bf16),
-                pltpu.VMEM((Z, part, cols), bf16),
-                pltpu.VMEM((parts, Z, part, cols), bf16),
-                pltpu.VMEM((parts, Z + 1, part, cols), bf16),
+                pltpu.VMEM((last_chunks, dp, cols, cw), bf16),
+                pltpu.VMEM((last_chunks, X, q, cols, cw), bf16),
+                pltpu.VMEM((last_chunks, X - 1, q, cols, cw), bf16),
+                pltpu.VMEM((last_chunks, X, q, cols, cw), bf16),
+                pltpu.VMEM((last_chunks, X - 1, q, cols, cw), bf16),
                 pltpu.VMEM((rows, cols), f32),
-                pltpu.VMEM((rows, cols), f32),
-                pltpu.VMEM((rows, cols), f32),
-                pltpu.VMEM((rows, cols), f32),
+                pltpu.VMEM((part, cols), f32),
+                pltpu.VMEM((part, cols), f32),
                 pltpu.VMEM((rows, cols), f32),
                 pltpu.VMEM((rows, cols), bf16),
                 pltpu.VMEM((rows, cols), bf16),
-                dma((6 + parts,)),
-                dma((5,)),
+                dma((4 + 3 * parts,)),
+                dma((3 + 2 * parts,)),
                 dma((2 + parts, Z)),
                 dma((2 + parts, Z)),
                 dma((2 + parts, Z)),
@@ -613,19 +737,21 @@
                 dma((2 + parts, 2)),
                 dma((2, 2 * X)),
                 dma((2, mp)),
-                dma((dp,)),
-                dma((mp, q)),
+                dma((X, q)),
+                dma((X, q)),
+                dma((X, q)),
+                dma((X - 1, q)),
                 dma((last_chunks, X, q)),
                 dma((last_chunks, X, q)),
                 dma((last_chunks, X, q)),
-                dma((last_chunks, X, q)),
+                dma((last_chunks, X - 1, q)),
                 dma((2 + X,)),
                 dma((2,)),
-                dma((pieces, Z)),
-                dma((pieces, Z)),
-                dma((pieces, Z)),
-                dma((pieces, Z + 1)),
-            ],
+                dma((n, Z)),
+                dma((n, Z)),
+                dma((n, Z)),
+                dma((n, Z + 1)),
+            ] + out_b + y_b + z_b,
             compiler_params=pltpu.CompilerParams(
                 collective_id=0, has_side_effects=True, vmem_limit_bytes=67043328
             ),

time: 329 us -> 297 us (0.903)
  Pallas kernels: 311 us -> 281 us
    pallas_call x1, Pallas kernels: 311 us -> 281 us  [per_device(): pl.pallas_call(functools.partial(kernel, dp, mp, rows, cols, parts, last_...]
where the time goes in v2:
time: 297 us; the launch traced here: 292 us
  Pallas kernels  281 us (95%)
  local copies, waits for them, and re-layouts  10.9 us (4%)
    pallas_call x1, Pallas kernels, per_device(): pl.pallas_call(functools.partial(kernel, dp, mp, rows, cols, parts, last_...  281 us
    unnamed x13, local copies, waits for them, and re-layouts  10.9 us

profile of v2, /device:TPU:12, one launch (start us, length us, event | category | flops | bytes accessed | tf_op | source)
XLA Modules:
  0.0 292.3 jit_solution(11850942298594447497)
XLA Ops:
  0.6 280.8 %shard_map.110 = (f32[1024,512]{1,0:T(8,128)}, f32[1024,512]{1,0:T(8,128)}, f32[1024,512]{1,0:T(8,128)}, f32[1024,512]{1,0:T(8,128)}, bf16[1024,512]{1,0:T(8,128)(2,1)}) custom-call(bf16[1024,512]{1,0:T(8,128)(2,1)} %bitcast.21, f32[1024,512]{1,0:T(8,128)} %bitcast.16, f32[1024,512]{1,0:T(8,128)} %bitcast.17, f32[1024,512]{1,0:T(8,128)} %bitcast.18, ...), custom_call_target="tpu_custom_call" | custom-call | tf_op jit(solution)/shard_map/pallas_call | solution.py:707
  281.5 0.0 copy-start.2
  281.5 3.2 %copy.17 = f32[1,1024,512]{2,1,0:T(8,128)} copy(f32[1,1024,512]{2,1,0:T(8,128)} %bitcast.15) | data formatting | bytes 4194304
  284.7 0.0 copy-done.2
  284.7 0.0 copy-start.1
  284.7 1.3 copy.18
  286.0 1.0 copy-done.1
  287.0 0.0 copy-start
  287.1 1.3 copy.19
  288.4 1.0 copy-done
  289.4 0.0 copy-start.3
  289.4 1.3 copy.20
  290.7 0.6 copy-done.3
  291.4 1.0 copy.21
Async XLA Ops:
  281.5 3.2 %copy-start.2 = (f32[1024,512]{1,0:T(8,128)S(1)}, f32[1024,512]{1,0:T(8,128)}, u32[]{:S(2)}) copy-start(f32[1024,512]{1,0:T(8,128)} %get-tuple-element.11) | copy-start | bytes 6291460
  284.7 2.3 copy-start.1
  287.0 2.3 copy-start
  289.4 2.0 copy-start.3

commit v3 on v2

--- a/solution.py
+++ b/solution.py
@@ -12,7 +12,7 @@
 epsilon = 1e-08
 bf16, f32 = jnp.bfloat16, jnp.float32
 MESH = pl.DeviceIdType.MESH
-PARTS, LAST = 2, 4
+PARTS, LAST, LAST_Z, EARLY = 2, 4, 1, 4
 Y_FIRST, Z_FIRST = 0, 1
 
 
@@ -24,7 +24,7 @@
         out[p].append((p, part // 2, part // 2, 0, cols, Y_FIRST))
     for h in range(last_chunks):
         cw = cols // last_chunks
-        out[parts - 1].append((parts - 1, 0, part, h * cw, cw, Y_FIRST))
+        out[parts - 1].append((parts - 1, 0, part, h * cw, cw, Z_FIRST if h < LAST_Z else Y_FIRST))
     return out
 
 
@@ -32,15 +32,17 @@
     pieces = scatter_pieces(rows, cols, parts, last_chunks)
     first_piece = [sum(len(x) for x in pieces[:p]) for p in range(parts)]
     n_pieces = sum(len(x) for x in pieces)
+    NAMED = len(refs) - 3 * n_pieces
     (grad, first, second, left_f, right_f, left_b, right_b,
      out_first, out_second, out_left, out_right, out_update,
-     gbuf, lbuf, rbuf, rrbuf, pbuf, ssend, r1buf, r2buf, u1buf, u2buf,
-     fac, mom1, mom2, acc, dbuf, bbuf,
+     gbuf, lbuf, rbuf, rrbuf, pbuf, ssend, r1buf, r2buf, u2buf,
+     fac_l, fac_r, mom1, mom2, acc, dbuf, bbuf,
      load_sem, store_sem, zs_up, zs_dn, zr, ys, yr, es, er, as_, ar,
-     rs1, rr1, rs2, rr2, us1, ur1, us2, ur2, ps, pr, bys, byr, bzs, bzr) = refs[:53]
-    out_bufs = refs[53:53 + n_pieces]
-    y_bufs = refs[53 + n_pieces:53 + 2 * n_pieces]
-    z_bufs = refs[53 + 2 * n_pieces:]
+     rs1, rr1, rs2, rr2, us1, ur1, us2, ur2, ps, pr, bys, byr, bzs, bzr) = refs[:NAMED]
+    out_bufs = refs[NAMED:NAMED + n_pieces]
+    y_bufs = refs[NAMED + n_pieces:NAMED + 2 * n_pieces]
+    z_bufs = refs[NAMED + 2 * n_pieces:]
+    u1buf = r1buf
     Z, q, X = dp // 2, rows // cols, mp // 2
     part, cw = rows // parts, cols // last_chunks
     d, m = lax.axis_index("dp"), lax.axis_index("mp")
@@ -69,7 +71,7 @@
         loop(n // size, lambda i: fn(pl.ds(pl.multiple_of(base + i * size, size), size)))
 
     loads = [
-        (grad, gbuf.at[d]), (right_b, rbuf.at[m]), (right_f, fac),
+        (grad, gbuf.at[d]), (right_b, rbuf.at[m]), (right_f, fac_r), (left_f, fac_l),
     ]
     loads += [(left_b.at[:, pl.ds(p * part, part)], lbuf.at[p, d]) for p in range(parts)]
     load = [pltpu.make_async_copy(a, b, load_sem.at[i]) for i, (a, b) in enumerate(loads)]
@@ -92,9 +94,8 @@
             for i, (a, b) in enumerate([(out_first, mom1), (out_second, mom2)])
         ]
 
-    load_left = pltpu.make_async_copy(left_f, fac, load_sem.at[3 + parts])
-    store_right = pltpu.make_async_copy(fac, out_right, store_sem.at[0])
-    store_left = pltpu.make_async_copy(fac, out_left, store_sem.at[1])
+    store_right = pltpu.make_async_copy(fac_r, out_right, store_sem.at[0])
+    store_left = pltpu.make_async_copy(fac_l, out_left, store_sem.at[1])
     store_update = pltpu.make_async_copy(dbuf, out_update, store_sem.at[2])
     for c in mom_loads(0):
         c.start()
@@ -195,8 +196,11 @@
         when(jnp.logical_and(zb == 0, z == last), lambda: extra(a, 0).wait_recv())
 
     def at_distance(s, fn):
-        when(z - s >= 0, lambda: fn(z - s))
-        when(jnp.logical_and(s > 0, z + s <= last), lambda: fn(z + s))
+        def side(j):
+            zb = z + (2 * j - 1) * s
+            ok = jnp.logical_and(zb >= 0, zb <= last)
+            when(jnp.logical_and(ok, jnp.logical_or(s > 0, j == 0)), lambda: fn(zb))
+        loop(2, side)
 
     def by_distance(fn, far_first=False):
         loop(Z, lambda i: at_distance(last - i if far_first else i, fn))
@@ -236,7 +240,7 @@
     load[1].wait()
     mp_first(0, rbuf, start)
     for p in range(parts):
-        load[3 + p].wait()
+        load[4 + p].wait()
 
     def far_slot(k):
         return lax.rem(k + X, X) - 1
@@ -334,9 +338,11 @@
             p_send(hb, hb, partner).wait_recv()
         to_chips(start)
 
-    def far_pair():
+    def far_relay():
         p_send(core, 0, partner).wait_recv()
         p_send(core, 0, partner).start()
+
+    def far_pair():
         p_send(1 - core, 0, partner).wait_recv()
 
     when(m == owner, own_pair)
@@ -411,18 +417,18 @@
             return pl.ds(pl.multiple_of(t.start + yy * n, t.size), t.size)
         for yy in range(2):
             def one(t, yy=yy):
-                acc[rows_of(t, yy), :] = back_term(zb * 2 + yy, piece, t)
+                acc[rows_of(t, yy), pl.ds(0, piece[4])] = back_term(zb * 2 + yy, piece, t)
             piece_tiles(piece, one)
 
         def add(slot):
             for yy in range(2):
                 def more(t, yy=yy):
-                    acc[rows_of(t, yy), :] += z_bufs[i][slot, yy, t, :].astype(f32)
+                    acc[rows_of(t, yy), pl.ds(0, piece[4])] += z_bufs[i][slot, yy, t, :].astype(f32)
                 piece_tiles(piece, more)
         z_arrivals(i, zb, add)
         for yy in range(2):
             def pack(t, yy=yy):
-                out_bufs[i][zb, yy, t, :] = acc[rows_of(t, yy), :].astype(bf16)
+                out_bufs[i][zb, yy, t, :] = acc[rows_of(t, yy), pl.ds(0, piece[4])].astype(bf16)
             piece_tiles(piece, pack)
         z_send(i, zb, out_bufs[i])
         when(zb == z, lambda: by_last(i).start())
@@ -491,13 +497,20 @@
         for c in mom_stores(p):
             c.start()
 
-    by_distance(lambda zb: r_term(zb * 2 + 1 - y))
+    def r_y_terms(near):
+        def one(zb):
+            db = zb * 2 + 1 - y
+            mine = lax.rem(lax.div(db, q), 2) == core
+            when(jnp.logical_xor(mine, near), lambda: r_term(db))
+        by_distance(one)
 
     def l_step(i):
         s = i + 1
         when(s == last, lambda: mp_relay(1, rrbuf))
         ag_step(2, s, then=3 if parts > 1 else None)
         when(jnp.logical_and(s == min(2, last), jnp.logical_and(chip == own_chip, m != owner)), near_pair)
+        when(s == 1, lambda: r_y_terms(True))
+        when(s == min(2, last), lambda: r_y_terms(False))
     loop(Z - 1, l_step)
     if parts > 1:
         y_sends(3, z, start)
@@ -518,15 +531,18 @@
                         total += r2buf[h, k - 1, sub, t, :].astype(f32)
                     where = pl.ds(pl.multiple_of(sub * cols + t.start, 128), 128)
                     c = pl.ds(h * cw, cw)
-                    fac[where, c] = decay_factor * fac[where, c] + (1.0 - decay_factor) * total
+                    fac_r[where, c] = decay_factor * fac_r[where, c] + (1.0 - decay_factor) * total
                 tiles(cols, 128, one)
+
+    def l_scale(t):
+        fac_l[t, :] = decay_factor * fac_l[t, :]
     load[2].wait()
-    r_final()
-    store_right.start()
+    load[3].wait()
+    tiles(rows, tile, l_scale)
 
     def l_term(db):
         def one(t):
-            fac[t, :] += (1.0 - decay_factor) * lax.dot_general(
+            fac_l[t, :] += (1.0 - decay_factor) * lax.dot_general(
                 gbuf[db, t, :], pbuf[db], (((1,), (1,)), ((), ())), preferred_element_type=f32
             )
         tiles(rows, tile, one)
@@ -534,12 +550,19 @@
     for p in range(1, parts):
         def both(i, p=p):
             s = i + 1
+            if p == 1:
+                when(jnp.logical_and(s == last, chip != own_chip), far_relay)
             ag_step(2 + p, s, then=3 + p if p + 1 < parts else None)
             for j, piece in numbered(p - 1):
                 scatter_step(j, piece, Z - s)
         loop(Z - 1, both)
         if p + 1 < parts:
             y_sends(3 + p, z, start)
+        if p == 1:
+            r_final()
+            store_right.start()
+            when(chip != own_chip, far_pair)
+            loop(EARLY, l_term)
         for j, piece in numbered(p - 1):
             scatter_step(j, piece, 0)
         zero_part()
@@ -547,22 +570,12 @@
             c.wait()
         for c in mom_loads(p):
             c.start()
-        if p == 1:
-            store_right.wait()
-            load_left.start()
         by_distance(lambda zb, p=p: m_term(p, zb * 2 + y))
         direction(p)
         scatter_first(p)
         for j, piece in numbered(p - 1):
             if piece[5] == Z_FIRST:
                 finish_z_first(j, piece)
-
-    when(chip != own_chip, far_pair)
-    load_left.wait()
-
-    def l_scale(t):
-        fac[t, :] = decay_factor * fac[t, :]
-    tiles(rows, tile, l_scale)
 
     def r_sent(db):
         mine = lax.rem(lax.div(db, q), 2) == core
@@ -625,19 +638,22 @@
                 dbuf[where, c] = total.astype(bf16)
             tiles(cols, 128, one)
 
-    done = 0
+    done = EARLY
     for tau in range(last_chunks + Z - 1):
         for h, (i, piece) in enumerate(numbered(parts - 1)):
+            late = 1 if piece[5] == Z_FIRST else 0
             if 0 <= tau - h <= last:
                 scatter_step(i, piece, last - (tau - h))
-                if tau - h == last:
-                    u_terms(h)
-        per = -(-dp // (last_chunks + Z - 2))
-        for db in range(done, min(done + per, dp)):
-            l_term(db)
-        done = min(done + per, dp)
-        if tau * per < dp <= (tau + 1) * per:
-            store_left.start()
+            if tau - h == last + late:
+                if late:
+                    finish_z_first(i, piece)
+                u_terms(h)
+        per = -(-(dp - EARLY) // (last_chunks + Z - 2))
+        if done < dp:
+            loop(min(per, dp - done), lambda k, done=done: l_term(done + k))
+            done = min(done + per, dp)
+            if done == dp:
+                store_left.start()
     for h in range(last_chunks):
         u_final(h)
     store_update.start()
@@ -680,8 +696,22 @@
             for xb in range(X):
                 u_near(h, xb, sub).wait_send()
                 when(xb != chip, lambda h=h, xb=xb, sub=sub: u_far(h, xb, sub).wait_send())
-    for c in mom_stores(parts - 1) + [store_left, store_update]:
+    for c in mom_stores(parts - 1) + [store_left, store_right, store_update]:
         c.wait()
+
+
+def write_out(*refs):
+    n = (len(refs) - 2) // 3
+    ins, outs, bufs, sem_in, sem_out = refs[:n], refs[n:2 * n], refs[2 * n:-2], refs[-2], refs[-1]
+    reads = [pltpu.make_async_copy(a, b, sem_in.at[i]) for i, (a, b) in enumerate(zip(ins, bufs))]
+    writes = [pltpu.make_async_copy(b, a, sem_out.at[i]) for i, (a, b) in enumerate(zip(outs, bufs))]
+    for c in reads:
+        c.start()
+    for r, w in zip(reads, writes):
+        r.wait()
+        w.start()
+    for w in writes:
+        w.wait()
 
 
 def solution(mesh):
@@ -718,8 +748,8 @@
                 pltpu.VMEM((last_chunks, dp, cols, cw), bf16),
                 pltpu.VMEM((last_chunks, X, q, cols, cw), bf16),
                 pltpu.VMEM((last_chunks, X - 1, q, cols, cw), bf16),
-                pltpu.VMEM((last_chunks, X, q, cols, cw), bf16),
                 pltpu.VMEM((last_chunks, X - 1, q, cols, cw), bf16),
+                pltpu.VMEM((rows, cols), f32),
                 pltpu.VMEM((rows, cols), f32),
                 pltpu.VMEM((part, cols), f32),
                 pltpu.VMEM((part, cols), f32),
@@ -756,6 +786,15 @@
                 collective_id=0, has_side_effects=True, vmem_limit_bytes=67043328
             ),
         )(*flat)
+        kinds = [jax.ShapeDtypeStruct(o.shape, o.dtype) for o in outs]
+        outs = pl.pallas_call(
+            write_out,
+            out_shape=kinds,
+            in_specs=[pl.BlockSpec(memory_space=pl.ANY)] * len(outs),
+            out_specs=[pl.BlockSpec(memory_space=pl.ANY)] * len(outs),
+            scratch_shapes=[pltpu.VMEM(o.shape, o.dtype) for o in outs] + [dma((len(outs),)), dma((len(outs),))],
+            compiler_params=pltpu.CompilerParams(vmem_limit_bytes=67043328),
+        )(*outs)
         return tuple(o.reshape((1,) + o.shape) for o in outs)
 
     return jax.shard_map(

time: 297 us -> 279 us (0.939)
  local copies, waits for them, and re-layouts: 10.9 us -> 0 us
  Pallas kernels: 281 us -> 276 us
    pallas_call x1, Pallas kernels: 281 us -> 268 us  [per_device(): pl.pallas_call(functools.partial(kernel, dp, mp, rows, cols, parts, last_...]
    unnamed x13 -> x0, local copies, waits for them, and re-layouts: 10.9 us -> none
    pallas_call x0 -> x1, Pallas kernels: none -> 7.31 us  [per_device(): pl.pallas_call(write_out, out_shape=kinds, in_specs=[pl.BlockSpec(memory_...]
where the time goes in v3:
time: 279 us; the launch traced here: 276 us
  Pallas kernels  276 us (99%)
    pallas_call x1, Pallas kernels, per_device(): pl.pallas_call(functools.partial(kernel, dp, mp, rows, cols, parts, last_...  268 us
    pallas_call x1, Pallas kernels, per_device(): pl.pallas_call(write_out, out_shape=kinds, in_specs=[pl.BlockSpec(memory_...  7.31 us

profile of v3, /device:TPU:12, one launch (start us, length us, event | category | flops | bytes accessed | tf_op | source)
XLA Modules:
  0.0 276.3 jit_solution(2881794495184923082)
XLA Ops:
  0.6 268.4 %shard_map.110 = (f32[1024,512]{1,0:T(8,128)}, f32[1024,512]{1,0:T(8,128)}, f32[1024,512]{1,0:T(8,128)}, f32[1024,512]{1,0:T(8,128)}, bf16[1024,512]{1,0:T(8,128)(2,1)}) custom-call(bf16[1024,512]{1,0:T(8,128)(2,1)} %bitcast.16, f32[1024,512]{1,0:T(8,128)} %bitcast.12, f32[1024,512]{1,0:T(8,128)} %bitcast.13, f32[1024,512]{1,0:T(8,128)} %bitcast.14, ...), custom_call_target="tpu_custom_call" | custom-call | tf_op jit(solution)/shard_map/pallas_call | solution.py:737
  269.0 7.3 %shard_map.111 = (f32[1024,512]{1,0:T(8,128)}, f32[1024,512]{1,0:T(8,128)}, f32[1024,512]{1,0:T(8,128)}, f32[1024,512]{1,0:T(8,128)}, bf16[1024,512]{1,0:T(8,128)(2,1)}) custom-call(f32[1024,512]{1,0:T(8,128)} %get-tuple-element.15.refs_0_, f32[1024,512]{1,0:T(8,128)} %get-tuple-element.16.refs_1_, f32[1024,512]{1,0:T(8,128)} %get-tuple-element.17.refs_2_, ...), custom_call_target="tpu_custom_call" | custom-call | tf_op jit(solution)/shard_map/pallas_call | solution.py:790

commit v4 on v3

--- a/solution.py
+++ b/solution.py
@@ -109,23 +109,18 @@
     along = (z > 0).astype(jnp.int32) + (z < last).astype(jnp.int32)
     pl.semaphore_wait(barrier, mp + along)
 
-    def view(a, b):
-        if a < 2:
-            return gbuf.at[b, pl.ds(a * (rows // 2), rows // 2), :]
-        return lbuf.at[a - 2, b]
-
     def half(a, b, hb):
         if a < 2:
             return gbuf.at[b, pl.ds(a * (rows // 2) + hb * (rows // 4), rows // 4), :]
         return lbuf.at[a - 2, b, pl.ds(hb * (cols // 2), cols // 2), :]
 
-    def up(a, zb):
-        blk = view(a, zb * 2 + y)
-        return send(blk, blk, zs_up.at[a, zb], zr.at[a, zb], (d + 2, m))
-
-    def dn(a, zb):
-        blk = view(a, zb * 2 + y)
-        return send(blk, blk, zs_dn.at[a, zb], zr.at[a, zb], (d - 2, m))
+    def up(a, zb, hb):
+        blk = half(a, zb * 2 + y, hb)
+        return send(blk, blk, zs_up.at[a, zb, hb], zr.at[a, zb, hb], (d + 2, m))
+
+    def dn(a, zb, hb):
+        blk = half(a, zb * 2 + y, hb)
+        return send(blk, blk, zs_dn.at[a, zb, hb], zr.at[a, zb, hb], (d - 2, m))
 
     def ysend(a, zb, hb):
         blk = half(a, zb * 2 + y, hb)
@@ -135,36 +130,45 @@
         blk = half(a, zb * 2 + (1 - y), hb)
         return send(blk, blk, ys.at[a, zb, hb], yr.at[a, zb, hb], (ynbr, m))
 
-    def extra(a, k):
+    def by_line(a):
+        return (0, 1) if a == 1 + parts else (1,)
+
+    def extra(a, k, hb):
         zb = 0 if k == 0 else last
-        blk = half(a, zb * 2 + (1 - y), 1)
-        return send(blk, blk, es.at[a, k], er.at[a, k], (d + 2, m) if k == 0 else (d - 2, m))
-
-    def y_second(zb):
+        blk = half(a, zb * 2 + (1 - y), hb)
+        return send(blk, blk, es.at[a, k, hb], er.at[a, k, hb], (d + 2, m) if k == 0 else (d - 2, m))
+
+    def over_y(a, zb, hb):
         inner = jnp.logical_and(zb > 0, zb < last)
         return jnp.logical_or(zb == z, inner)
 
     def y_sends(a, zb, op):
-        when(y_second(zb), lambda: op(ysend(a, zb, 1)))
-        op(ysend(a, zb, 0))
+        for hb in (1, 0):
+            if hb in by_line(a):
+                when(over_y(a, zb, hb), lambda hb=hb: op(ysend(a, zb, hb)))
+            else:
+                op(ysend(a, zb, hb))
 
     def start(c):
         c.start()
 
     def ag_own(a):
-        when(z < last, lambda: up(a, z).start())
-        when(z > 0, lambda: dn(a, z).start())
+        for hb in range(2):
+            when(z < last, lambda: up(a, z, hb).start())
+            when(z > 0, lambda: dn(a, z, hb).start())
 
     def ag_step(a, s, then=None):
         below, above = z - s, z + s
 
         def from_below():
-            up(a, below).wait_recv()
-            when(z < last, lambda: up(a, below).start())
+            for hb in range(2):
+                up(a, below, hb).wait_recv()
+                when(z < last, lambda hb=hb: up(a, below, hb).start())
 
         def from_above():
-            dn(a, above).wait_recv()
-            when(z > 0, lambda: dn(a, above).start())
+            for hb in range(2):
+                dn(a, above, hb).wait_recv()
+                when(z > 0, lambda hb=hb: dn(a, above, hb).start())
 
         when(below >= 0, from_below)
         when(above <= last, from_above)
@@ -172,28 +176,35 @@
         when(above <= last, lambda: y_sends(a, above, start))
 
         def extra_dn():
-            when(z == last, lambda: yrecv_desc(a, z, 1).wait_recv())
-            when(z < last, lambda: extra(a, 1).wait_recv())
-            extra(a, 1).start()
+            for hb in by_line(a):
+                when(z == last, lambda hb=hb: yrecv_desc(a, z, hb).wait_recv())
+                when(z < last, lambda hb=hb: extra(a, 1, hb).wait_recv())
+                extra(a, 1, hb).start()
             if then is not None:
-                dn(then, z).start()
+                for hb in range(2):
+                    dn(then, z, hb).start()
 
         def extra_up():
-            when(z == 0, lambda: yrecv_desc(a, z, 1).wait_recv())
-            when(z > 0, lambda: extra(a, 0).wait_recv())
-            extra(a, 0).start()
+            for hb in by_line(a):
+                when(z == 0, lambda hb=hb: yrecv_desc(a, z, hb).wait_recv())
+                when(z > 0, lambda hb=hb: extra(a, 0, hb).wait_recv())
+                extra(a, 0, hb).start()
             if then is not None:
-                up(then, z).start()
+                for hb in range(2):
+                    up(then, z, hb).start()
 
         when(jnp.logical_and(z == Z - s, z > 0), extra_dn)
         when(jnp.logical_and(z == s - 1, z < last), extra_up)
 
     def wait_y(a, zb):
-        yrecv_desc(a, zb, 0).wait_recv()
         inner = jnp.logical_and(zb > 0, zb < last)
-        when(inner, lambda: yrecv_desc(a, zb, 1).wait_recv())
-        when(jnp.logical_and(zb == last, z == 0), lambda: extra(a, 1).wait_recv())
-        when(jnp.logical_and(zb == 0, z == last), lambda: extra(a, 0).wait_recv())
+        for hb in range(2):
+            if hb in by_line(a):
+                when(inner, lambda hb=hb: yrecv_desc(a, zb, hb).wait_recv())
+                when(jnp.logical_and(zb == last, z == 0), lambda hb=hb: extra(a, 1, hb).wait_recv())
+                when(jnp.logical_and(zb == 0, z == last), lambda hb=hb: extra(a, 0, hb).wait_recv())
+            else:
+                yrecv_desc(a, zb, hb).wait_recv()
 
     def at_distance(s, fn):
         def side(j):
@@ -447,6 +458,8 @@
     def scatter_first(p):
         for i, piece in numbered(p):
             if piece[5] == Z_FIRST:
+                if p == parts - 1:
+                    scatter_step(i, piece, last)
                 continue
 
             def one_block(zb, i=i, piece=piece):
@@ -562,7 +575,7 @@
             r_final()
             store_right.start()
             when(chip != own_chip, far_pair)
-            loop(EARLY, l_term)
+            when(jnp.logical_or(z == 0, z == last), lambda: loop(EARLY, l_term))
         for j, piece in numbered(p - 1):
             scatter_step(j, piece, 0)
         zero_part()
@@ -601,11 +614,21 @@
 
     def u_dot(h, db):
         c = pl.ds(h * cw, cw)
-        total = None
-        for p in range(parts):
-            term = jnp.dot(lbuf[p, db], bbuf[pl.ds(p * part, part), c], preferred_element_type=f32)
-            total = term if total is None else total + term
-        return total
+        p = parts - 1
+        term = jnp.dot(lbuf[p, db], bbuf[pl.ds(p * part, part), c], preferred_element_type=f32)
+        return ssend[h, db].astype(f32) + term
+
+    def u_before():
+        def one(db):
+            for h0 in range(0, last_chunks, 2):
+                c = pl.ds(h0 * cw, 2 * cw)
+                total = None
+                for p in range(parts - 1):
+                    term = jnp.dot(lbuf[p, db], bbuf[pl.ds(p * part, part), c], preferred_element_type=f32)
+                    total = term if total is None else total + term
+                for h in range(2):
+                    ssend[h0 + h, db] = total[:, h * cw:(h + 1) * cw].astype(bf16)
+        loop(dp, one)
 
     def u_terms(h):
         def near(i):
@@ -639,16 +662,25 @@
             tiles(cols, 128, one)
 
     done = EARLY
+    wide = numbered(parts - 1)
+    per = -(-(dp - EARLY) // (last_chunks + Z - 2))
     for tau in range(last_chunks + Z - 1):
-        for h, (i, piece) in enumerate(numbered(parts - 1)):
-            late = 1 if piece[5] == Z_FIRST else 0
-            if 0 <= tau - h <= last:
+        for h, (i, piece) in enumerate(wide):
+            if 0 <= tau - h < last and not (piece[5] == Z_FIRST and tau == 0):
                 scatter_step(i, piece, last - (tau - h))
-            if tau - h == last + late:
-                if late:
-                    finish_z_first(i, piece)
+        if tau == 1:
+            u_before()
+        if tau == 2:
+            when(jnp.logical_and(z > 0, z < last), lambda: loop(EARLY, l_term))
+        for h, (i, piece) in enumerate(wide):
+            z_first = piece[5] == Z_FIRST
+            if tau - h == last:
+                scatter_step(i, piece, 0)
+                if not z_first:
+                    u_terms(h)
+            if z_first and tau == min(h + last + 2, last_chunks + Z - 2):
+                finish_z_first(i, piece)
                 u_terms(h)
-        per = -(-(dp - EARLY) // (last_chunks + Z - 2))
         if done < dp:
             loop(min(per, dp - done), lambda k, done=done: l_term(done + k))
             done = min(done + per, dp)
@@ -660,12 +692,14 @@
 
     for a in range(2 + parts):
         def sent(i, a=a):
-            when(jnp.logical_and(z < last, i <= z), lambda: up(a, i).wait_send())
-            when(jnp.logical_and(z > 0, i >= z), lambda: dn(a, i).wait_send())
+            for hb in range(2):
+                when(jnp.logical_and(z < last, i <= z), lambda: up(a, i, hb).wait_send())
+                when(jnp.logical_and(z > 0, i >= z), lambda: dn(a, i, hb).wait_send())
             y_sends(a, i, lambda c: c.wait_send())
         loop(Z, sent)
-        when(z > 0, lambda a=a: extra(a, 1).wait_send())
-        when(z < last, lambda a=a: extra(a, 0).wait_send())
+        for hb in by_line(a):
+            when(z > 0, lambda: extra(a, 1, hb).wait_send())
+            when(z < last, lambda: extra(a, 0, hb).wait_send())
     mp_sent(0, rbuf)
     mp_sent(1, rrbuf)
 
@@ -758,13 +792,13 @@
                 pltpu.VMEM((rows, cols), bf16),
                 dma((4 + 3 * parts,)),
                 dma((3 + 2 * parts,)),
-                dma((2 + parts, Z)),
-                dma((2 + parts, Z)),
-                dma((2 + parts, Z)),
                 dma((2 + parts, Z, 2)),
                 dma((2 + parts, Z, 2)),
-                dma((2 + parts, 2)),
-                dma((2 + parts, 2)),
+                dma((2 + parts, Z, 2)),
+                dma((2 + parts, Z, 2)),
+                dma((2 + parts, Z, 2)),
+                dma((2 + parts, 2, 2)),
+                dma((2 + parts, 2, 2)),
                 dma((2, 2 * X)),
                 dma((2, mp)),
                 dma((X, q)),

time: 279 us -> 279 us (level)
  no operation moved by 1% of the time
where the time goes in v4:
time: 279 us; the launch traced here: 278 us
  Pallas kernels  277 us (99%)
    pallas_call x1, Pallas kernels, per_device(): pl.pallas_call(functools.partial(kernel, dp, mp, rows, cols, parts, last_...  270 us
    pallas_call x1, Pallas kernels, per_device(): pl.pallas_call(write_out, out_shape=kinds, in_specs=[pl.BlockSpec(memory_...  7.31 us

profile of v4, /device:TPU:12, one launch (start us, length us, event | category | flops | bytes accessed | tf_op | source)
XLA Modules:
  0.0 278.1 jit_solution(10978788863786930933)
XLA Ops:
  0.6 270.0 %shard_map.110 = (f32[1024,512]{1,0:T(8,128)}, f32[1024,512]{1,0:T(8,128)}, f32[1024,512]{1,0:T(8,128)}, f32[1024,512]{1,0:T(8,128)}, bf16[1024,512]{1,0:T(8,128)(2,1)}) custom-call(bf16[1024,512]{1,0:T(8,128)(2,1)} %bitcast.16, f32[1024,512]{1,0:T(8,128)} %bitcast.12, f32[1024,512]{1,0:T(8,128)} %bitcast.13, f32[1024,512]{1,0:T(8,128)} %bitcast.14, ...), custom_call_target="tpu_custom_call" | custom-call | tf_op jit(solution)/shard_map/pallas_call | solution.py:771
  270.7 7.3 %shard_map.111 = (f32[1024,512]{1,0:T(8,128)}, f32[1024,512]{1,0:T(8,128)}, f32[1024,512]{1,0:T(8,128)}, f32[1024,512]{1,0:T(8,128)}, bf16[1024,512]{1,0:T(8,128)(2,1)}) custom-call(f32[1024,512]{1,0:T(8,128)} %get-tuple-element.15.refs_0_, f32[1024,512]{1,0:T(8,128)} %get-tuple-element.16.refs_1_, f32[1024,512]{1,0:T(8,128)} %get-tuple-element.17.refs_2_, ...), custom_call_target="tpu_custom_call" | custom-call | tf_op jit(solution)/shard_map/pallas_call | solution.py:824

commit v5 on v4

--- a/solution.py
+++ b/solution.py
@@ -131,7 +131,7 @@
         return send(blk, blk, ys.at[a, zb, hb], yr.at[a, zb, hb], (ynbr, m))
 
     def by_line(a):
-        return (0, 1) if a == 1 + parts else (1,)
+        return (1,)
 
     def extra(a, k, hb):
         zb = 0 if k == 0 else last
@@ -360,7 +360,7 @@
 
     def back_term(db, piece, t):
         p, r0, _, c0, w, _ = piece
-        off = pl.multiple_of(lax.rem(db, q) * cols + c0, w)
+        off = pl.multiple_of(lax.rem(db, q) * cols + c0, 128)
         rhs = rbuf[lax.div(db, q), pl.ds(off, w), :]
         mine = pl.ds(pl.multiple_of(t.start + (p * part + r0), t.size), t.size)
         return lax.dot_general(
@@ -456,18 +456,29 @@
         return list(enumerate(pieces[p], first_piece[p]))
 
     def scatter_first(p):
+        groups = []
         for i, piece in numbered(p):
             if piece[5] == Z_FIRST:
                 if p == parts - 1:
                     scatter_step(i, piece, last)
-                continue
-
-            def one_block(zb, i=i, piece=piece):
+            elif len(groups) > 1 and len(groups[-1]) == 1:
+                groups[-1].append((i, piece))
+            else:
+                groups.append([(i, piece)])
+        for group in groups:
+            p0, r0, nr, c0, w, kind = group[0][1]
+            both = (p0, r0, nr, c0, w * len(group), kind)
+
+            def one_block(zb, group=group, both=both, w=w):
                 def one(t):
-                    out_bufs[i][zb, t, :] = back_term(zb * 2 + 1 - y, piece, t).astype(bf16)
-                piece_tiles(piece, one)
-                by_send(i, zb).start()
+                    value = back_term(zb * 2 + 1 - y, both, t).astype(bf16)
+                    for j, (i, _) in enumerate(group):
+                        out_bufs[i][zb, t, :] = value[:, j * w:(j + 1) * w]
+                piece_tiles(both, one)
+                by_send(group[0][0], zb).start()
             by_distance(one_block, far_first=True)
+            for i, _ in group[1:]:
+                by_distance(lambda zb, i=i: by_send(i, zb).start(), far_first=True)
 
     def scatter_step(i, piece, s):
         fn = line_z_first if piece[5] == Z_FIRST else line_y_first
@@ -663,24 +674,33 @@
 
     done = EARLY
     wide = numbered(parts - 1)
-    per = -(-(dp - EARLY) // (last_chunks + Z - 2))
-    for tau in range(last_chunks + Z - 1):
+    steady = [i for i, piece in wide if piece[5] == Y_FIRST]
+    taus = len(steady) + Z - 1
+    per = -(-(dp - EARLY) // (taus - 1))
+
+    def when_due(i, piece, t):
+        if piece[5] == Y_FIRST:
+            return steady.index(i) + last - t
+        return ((last - t) * (taus - 3) * 2 + last) // (2 * last)
+
+    for tau in range(taus):
         for h, (i, piece) in enumerate(wide):
-            if 0 <= tau - h < last and not (piece[5] == Z_FIRST and tau == 0):
-                scatter_step(i, piece, last - (tau - h))
+            for t in range(last, 0, -1):
+                if when_due(i, piece, t) == tau and not (piece[5] == Z_FIRST and t == last):
+                    scatter_step(i, piece, t)
         if tau == 1:
             u_before()
         if tau == 2:
             when(jnp.logical_and(z > 0, z < last), lambda: loop(EARLY, l_term))
         for h, (i, piece) in enumerate(wide):
             z_first = piece[5] == Z_FIRST
-            if tau - h == last:
+            if z_first and tau == when_due(i, piece, 0) + 1:
+                finish_z_first(i, piece)
+                u_terms(h)
+            if when_due(i, piece, 0) == tau:
                 scatter_step(i, piece, 0)
                 if not z_first:
                     u_terms(h)
-            if z_first and tau == min(h + last + 2, last_chunks + Z - 2):
-                finish_z_first(i, piece)
-                u_terms(h)
         if done < dp:
             loop(min(per, dp - done), lambda k, done=done: l_term(done + k))
             done = min(done + per, dp)

time: 279 us -> 270 us (0.968)
  Pallas kernels: 277 us -> 268 us
    pallas_call x1, Pallas kernels: 270 us -> 261 us  [per_device(): pl.pallas_call(functools.partial(kernel, dp, mp, rows, cols, parts, last_...]
where the time goes in v5:
time: 270 us; the launch traced here: 269 us
  Pallas kernels  268 us (99%)
    pallas_call x1, Pallas kernels, per_device(): pl.pallas_call(functools.partial(kernel, dp, mp, rows, cols, parts, last_...  261 us
    pallas_call x1, Pallas kernels, per_device(): pl.pallas_call(write_out, out_shape=kinds, in_specs=[pl.BlockSpec(memory_...  7.31 us

profile of v5, /device:TPU:12, one launch (start us, length us, event | category | flops | bytes accessed | tf_op | source)
XLA Modules:
  0.0 269.1 jit_solution(2015708922836045003)
XLA Ops:
  0.6 261.0 %shard_map.110 = (f32[1024,512]{1,0:T(8,128)}, f32[1024,512]{1,0:T(8,128)}, f32[1024,512]{1,0:T(8,128)}, f32[1024,512]{1,0:T(8,128)}, bf16[1024,512]{1,0:T(8,128)(2,1)}) custom-call(bf16[1024,512]{1,0:T(8,128)(2,1)} %bitcast.16, f32[1024,512]{1,0:T(8,128)} %bitcast.12, f32[1024,512]{1,0:T(8,128)} %bitcast.13, f32[1024,512]{1,0:T(8,128)} %bitcast.14, ...), custom_call_target="tpu_custom_call" | custom-call | tf_op jit(solution)/shard_map/pallas_call | solution.py:791
  261.6 7.3 %shard_map.111 = (f32[1024,512]{1,0:T(8,128)}, f32[1024,512]{1,0:T(8,128)}, f32[1024,512]{1,0:T(8,128)}, f32[1024,512]{1,0:T(8,128)}, bf16[1024,512]{1,0:T(8,128)(2,1)}) custom-call(f32[1024,512]{1,0:T(8,128)} %get-tuple-element.15.refs_0_, f32[1024,512]{1,0:T(8,128)} %get-tuple-element.16.refs_1_, f32[1024,512]{1,0:T(8,128)} %get-tuple-element.17.refs_2_, ...), custom_call_target="tpu_custom_call" | custom-call | tf_op jit(solution)/shard_map/pallas_call | solution.py:844

commit v6 on v5

--- a/solution.py
+++ b/solution.py
@@ -14,6 +14,7 @@
 MESH = pl.DeviceIdType.MESH
 PARTS, LAST, LAST_Z, EARLY = 2, 4, 1, 4
 Y_FIRST, Z_FIRST = 0, 1
+PIECE_US, HOP_US, CHAIN_US, Z_HOP_US, L_FROM = 11, 3, 8, 8, 3
 
 
 def scatter_pieces(rows, cols, parts, last_chunks):
@@ -142,12 +143,15 @@
         inner = jnp.logical_and(zb > 0, zb < last)
         return jnp.logical_or(zb == z, inner)
 
+    def y_half(a, zb, hb, op):
+        if hb in by_line(a):
+            when(over_y(a, zb, hb), lambda: op(ysend(a, zb, hb)))
+        else:
+            op(ysend(a, zb, hb))
+
     def y_sends(a, zb, op):
         for hb in (1, 0):
-            if hb in by_line(a):
-                when(over_y(a, zb, hb), lambda hb=hb: op(ysend(a, zb, hb)))
-            else:
-                op(ysend(a, zb, hb))
+            y_half(a, zb, hb, op)
 
     def start(c):
         c.start()
@@ -164,16 +168,16 @@
             for hb in range(2):
                 up(a, below, hb).wait_recv()
                 when(z < last, lambda hb=hb: up(a, below, hb).start())
+                y_half(a, below, hb, start)
 
         def from_above():
             for hb in range(2):
                 dn(a, above, hb).wait_recv()
                 when(z > 0, lambda hb=hb: dn(a, above, hb).start())
+                y_half(a, above, hb, start)
 
         when(below >= 0, from_below)
         when(above <= last, from_above)
-        when(below >= 0, lambda: y_sends(a, below, start))
-        when(above <= last, lambda: y_sends(a, above, start))
 
         def extra_dn():
             for hb in by_line(a):
@@ -574,11 +578,11 @@
     for p in range(1, parts):
         def both(i, p=p):
             s = i + 1
+            for j, piece in numbered(p - 1):
+                scatter_step(j, piece, Z - s)
+            ag_step(2 + p, s, then=3 + p if p + 1 < parts else None)
             if p == 1:
                 when(jnp.logical_and(s == last, chip != own_chip), far_relay)
-            ag_step(2 + p, s, then=3 + p if p + 1 < parts else None)
-            for j, piece in numbered(p - 1):
-                scatter_step(j, piece, Z - s)
         loop(Z - 1, both)
         if p + 1 < parts:
             y_sends(3 + p, z, start)
@@ -586,7 +590,7 @@
             r_final()
             store_right.start()
             when(chip != own_chip, far_pair)
-            when(jnp.logical_or(z == 0, z == last), lambda: loop(EARLY, l_term))
+            loop(EARLY, l_term)
         for j, piece in numbered(p - 1):
             scatter_step(j, piece, 0)
         zero_part()
@@ -672,40 +676,37 @@
                 dbuf[where, c] = total.astype(bf16)
             tiles(cols, 128, one)
 
+    steps, k = [], 0
+    for h, (i, piece) in enumerate(numbered(parts - 1)):
+        for t in range(last, -1, -1):
+            if piece[5] == Y_FIRST:
+                due = PIECE_US * k + HOP_US * (last - t) + 5 + (CHAIN_US if t == 0 else 0)
+            else:
+                due = Z_HOP_US * (last - t)
+            if piece[5] == Y_FIRST or t < last:
+                steps.append((due, len(steps), h, i, piece, t))
+        if piece[5] == Z_FIRST:
+            steps.append((Z_HOP_US * last + 10, len(steps), h, i, piece, -1))
+        else:
+            k += 1
+    steps.sort(key=lambda e: e[:2])
+    u_before()
     done = EARLY
-    wide = numbered(parts - 1)
-    steady = [i for i, piece in wide if piece[5] == Y_FIRST]
-    taus = len(steady) + Z - 1
-    per = -(-(dp - EARLY) // (taus - 1))
-
-    def when_due(i, piece, t):
-        if piece[5] == Y_FIRST:
-            return steady.index(i) + last - t
-        return ((last - t) * (taus - 3) * 2 + last) // (2 * last)
-
-    for tau in range(taus):
-        for h, (i, piece) in enumerate(wide):
-            for t in range(last, 0, -1):
-                if when_due(i, piece, t) == tau and not (piece[5] == Z_FIRST and t == last):
-                    scatter_step(i, piece, t)
-        if tau == 1:
-            u_before()
-        if tau == 2:
-            when(jnp.logical_and(z > 0, z < last), lambda: loop(EARLY, l_term))
-        for h, (i, piece) in enumerate(wide):
-            z_first = piece[5] == Z_FIRST
-            if z_first and tau == when_due(i, piece, 0) + 1:
-                finish_z_first(i, piece)
-                u_terms(h)
-            if when_due(i, piece, 0) == tau:
-                scatter_step(i, piece, 0)
-                if not z_first:
-                    u_terms(h)
-        if done < dp:
-            loop(min(per, dp - done), lambda k, done=done: l_term(done + k))
-            done = min(done + per, dp)
+    for n, (_, _, h, i, piece, t) in enumerate(steps):
+        if t >= 0:
+            scatter_step(i, piece, t)
+        else:
+            finish_z_first(i, piece)
+        if t == (-1 if piece[5] == Z_FIRST else 0):
+            u_terms(h)
+        if n >= L_FROM and done < dp:
+            l_term(done)
+            done += 1
             if done == dp:
                 store_left.start()
+    if done < dp:
+        loop(dp - done, lambda k, done=done: l_term(done + k))
+        store_left.start()
     for h in range(last_chunks):
         u_final(h)
     store_update.start()

time: 270 us -> 266 us (0.985)
  Pallas kernels: 268 us -> 262 us
    pallas_call x1, Pallas kernels: 261 us -> 255 us  [per_device(): pl.pallas_call(functools.partial(kernel, dp, mp, rows, cols, parts, last_...]
where the time goes in v6:
time: 266 us; the launch traced here: 263 us
  Pallas kernels  262 us (98%)
    pallas_call x1, Pallas kernels, per_device(): pl.pallas_call(functools.partial(kernel, dp, mp, rows, cols, parts, last_...  255 us
    pallas_call x1, Pallas kernels, per_device(): pl.pallas_call(write_out, out_shape=kinds, in_specs=[pl.BlockSpec(memory_...  7.31 us

profile of v6, /device:TPU:12, one launch (start us, length us, event | category | flops | bytes accessed | tf_op | source)
XLA Modules:
  0.0 263.0 jit_solution(5881699223697685186)
XLA Ops:
  0.6 255.1 %shard_map.110 = (f32[1024,512]{1,0:T(8,128)}, f32[1024,512]{1,0:T(8,128)}, f32[1024,512]{1,0:T(8,128)}, f32[1024,512]{1,0:T(8,128)}, bf16[1024,512]{1,0:T(8,128)(2,1)}) custom-call(bf16[1024,512]{1,0:T(8,128)(2,1)} %bitcast.16, f32[1024,512]{1,0:T(8,128)} %bitcast.12, f32[1024,512]{1,0:T(8,128)} %bitcast.13, f32[1024,512]{1,0:T(8,128)} %bitcast.14, ...), custom_call_target="tpu_custom_call" | custom-call | tf_op jit(solution)/shard_map/pallas_call | solution.py:792
  255.7 7.3 %shard_map.111 = (f32[1024,512]{1,0:T(8,128)}, f32[1024,512]{1,0:T(8,128)}, f32[1024,512]{1,0:T(8,128)}, f32[1024,512]{1,0:T(8,128)}, bf16[1024,512]{1,0:T(8,128)(2,1)}) custom-call(f32[1024,512]{1,0:T(8,128)} %get-tuple-element.15.refs_0_, f32[1024,512]{1,0:T(8,128)} %get-tuple-element.16.refs_1_, f32[1024,512]{1,0:T(8,128)} %get-tuple-element.17.refs_2_, ...), custom_call_target="tpu_custom_call" | custom-call | tf_op jit(solution)/shard_map/pallas_call | solution.py:845

commit v7 on v6

--- a/solution.py
+++ b/solution.py
@@ -14,7 +14,7 @@
 MESH = pl.DeviceIdType.MESH
 PARTS, LAST, LAST_Z, EARLY = 2, 4, 1, 4
 Y_FIRST, Z_FIRST = 0, 1
-PIECE_US, HOP_US, CHAIN_US, Z_HOP_US, L_FROM = 11, 3, 8, 8, 3
+PIECE_US, HOP_US, CHAIN_US, Z_HOP_US, L_FROM, U_AT = 11, 3, 8, 8, 3, 2
 
 
 def scatter_pieces(rows, cols, parts, last_chunks):
@@ -490,23 +490,26 @@
 
     mom_tile = min(128, part)
 
+    def held(p, t):
+        return pl.ds(pl.multiple_of(t.start + min(p, 1) * part, t.size), t.size)
+
     def m_term(p, db):
         rhs = sub_rows(rrbuf, db)
         def one(t):
-            acc[t, :] += lax.dot_general(
+            acc[held(p, t), :] += lax.dot_general(
                 lbuf[p, db, :, t], rhs[...], (((0,), (0,)), ((), ())), preferred_element_type=f32
             )
         tiles(part, tile, one)
 
     def zero_part():
         def one(t):
-            acc[t, :] = jnp.zeros((tile, cols), f32)
+            acc[held(1, t), :] = jnp.zeros((tile, cols), f32)
         tiles(part, tile, one)
 
     def moments(p):
         def one(t):
             w = pl.ds(pl.multiple_of(t.start + p * part, mom_tile), mom_tile)
-            rot = acc[t, :]
+            rot = acc[held(p, t), :]
             new1 = decay_moment * mom1[t, :] + (1.0 - decay_moment) * rot
             new2 = decay_moment * mom2[t, :] + (1.0 - decay_moment) * rot * rot
             mom1[t, :] = new1
@@ -591,14 +594,14 @@
             store_right.start()
             when(chip != own_chip, far_pair)
             loop(EARLY, l_term)
+        zero_part()
+        by_distance(lambda zb, p=p: m_term(p, zb * 2 + y))
         for j, piece in numbered(p - 1):
             scatter_step(j, piece, 0)
-        zero_part()
         for c in mom_stores(p - 1):
             c.wait()
         for c in mom_loads(p):
             c.start()
-        by_distance(lambda zb, p=p: m_term(p, zb * 2 + y))
         direction(p)
         scatter_first(p)
         for j, piece in numbered(p - 1):
@@ -690,9 +693,10 @@
         else:
             k += 1
     steps.sort(key=lambda e: e[:2])
-    u_before()
     done = EARLY
     for n, (_, _, h, i, piece, t) in enumerate(steps):
+        if n == U_AT:
+            u_before()
         if t >= 0:
             scatter_step(i, piece, t)
         else:

time: 266 us -> 264 us (level)
  no operation moved by 1% of the time
where the time goes in v7:
time: 264 us; the launch traced here: 261 us
  Pallas kernels  260 us (98%)
    pallas_call x1, Pallas kernels, per_device(): pl.pallas_call(functools.partial(kernel, dp, mp, rows, cols, parts, last_...  253 us
    pallas_call x1, Pallas kernels, per_device(): pl.pallas_call(write_out, out_shape=kinds, in_specs=[pl.BlockSpec(memory_...  7.31 us

profile of v7, /device:TPU:12, one launch (start us, length us, event | category | flops | bytes accessed | tf_op | source)
XLA Modules:
  0.0 260.7 jit_solution(12438676571339648375)
XLA Ops:
  0.6 252.8 %shard_map.110 = (f32[1024,512]{1,0:T(8,128)}, f32[1024,512]{1,0:T(8,128)}, f32[1024,512]{1,0:T(8,128)}, f32[1024,512]{1,0:T(8,128)}, bf16[1024,512]{1,0:T(8,128)(2,1)}) custom-call(bf16[1024,512]{1,0:T(8,128)(2,1)} %bitcast.16, f32[1024,512]{1,0:T(8,128)} %bitcast.12, f32[1024,512]{1,0:T(8,128)} %bitcast.13, f32[1024,512]{1,0:T(8,128)} %bitcast.14, ...), custom_call_target="tpu_custom_call" | custom-call | tf_op jit(solution)/shard_map/pallas_call | solution.py:796
  253.4 7.3 %shard_map.111 = (f32[1024,512]{1,0:T(8,128)}, f32[1024,512]{1,0:T(8,128)}, f32[1024,512]{1,0:T(8,128)}, f32[1024,512]{1,0:T(8,128)}, bf16[1024,512]{1,0:T(8,128)(2,1)}) custom-call(f32[1024,512]{1,0:T(8,128)} %get-tuple-element.15.refs_0_, f32[1024,512]{1,0:T(8,128)} %get-tuple-element.16.refs_1_, f32[1024,512]{1,0:T(8,128)} %get-tuple-element.17.refs_2_, ...), custom_call_target="tpu_custom_call" | custom-call | tf_op jit(solution)/shard_map/pallas_call | solution.py:849
